TPU v7x, 32 devices: a whole 2x2x4 slice. The times are simulated.
32 devices in a mesh: gx: 2 (over x), gy: 4 (over z), gz: 4 (over y, core).
Axes of the slice: x: 2, y: 2, z: 4, core: 2. Of those that a mesh axis runs over, the one named last changes fastest.
Arguments:
- source_points: float32 [1024, 3, 384], P(('gx', 'gy', 'gz'))
- target_points: float32 [1024, 3, 384], P(('gx', 'gy', 'gz'))
- pair_scans: int32 [1024, 2], P(('gx', 'gy', 'gz')), may hold values from 0 to 127, as said below
- point_counts: int32 [1024, 2], P(('gx', 'gy', 'gz')), may hold values from 48 to 384
- live_tasks: int32 [32], P(('gx', 'gy', 'gz')), may hold values from 1 to 32, as said below
- pose_init: float32 [128, 12], P(('gx', 'gy', 'gz')), may hold values from -1 to 1, as said below
- gauge: int32 [1], replicated, may hold values from 0 to 127
Outputs:
- poses_out: float32 [128, 12], P(('gx', 'gy', 'gz'))
Inputs may be any that keep to these rules, and one draw needn't show every extreme that they name: pair_scans[p, 0] is one of the 4 scans of the device that holds slot p (scans are numbered 4 a device, in device order); pair_scans[p, 1] differs from pair_scans[p, 0]. `live_tasks`: the live slots of a device are its first ones; some device has 32 live slots. `pose_init`: each rotation is orthonormal.
All inputs are finite; a program needn't handle non-finite values.
Results may differ from a plain program's by a relative error of at most 0.0003.
Values sent between devices are 32-bit elements; how exact they have to be, the bound alone decides.
No kernel may reach another device: no remote copies, remote signals or barrier semaphores. Data moves between devices by JAX's collectives and lax.ppermute only.
A program may use at most 64 MiB of HBM per device.

v0:
```python
import jax
import jax.numpy as jnp
from jax import lax
from jax.experimental import pallas as pl
from jax.experimental.pallas import tpu as pltpu
from jax.sharding import PartitionSpec as P

AXES = ("gx", "gy", "gz")
ITERS = 2
SPREAD = 2.0
DAMPING = 1.0
FLOOR = -1e30
LOG2E = 1.4426950408889634
LIFT = 100.0
TINY = 2.0**-100
UNROLL = 8
STEP = 8
SCALE = 2.0 * SPREAD * LOG2E
LANES = 128


def halves(value):
    first = value.astype(jnp.bfloat16).astype(jnp.float32)
    rest = value - first
    second = rest.astype(jnp.bfloat16).astype(jnp.float32)
    return first, second, rest - second


def moved(points_ref, task, pose, row3, width):
    reps = width // LANES

    def column(index):
        a, b, c = (pose(index, r) for r in range(3))
        col = jnp.where(row3 == 0, a, jnp.where(row3 == 1, b, c))
        return jnp.concatenate([col] * reps, axis=1)

    out = column(3)
    for axis in range(3):
        row = jnp.broadcast_to(points_ref[axis, pl.ds(task, 1), :], (8, width))
        out = out + column(axis) * row
    return out


def operands(task, pose_of, ids_ref, counts_ref, src_ref, tgt_ref):
    width = src_ref.shape[2]
    sub = lax.broadcasted_iota(jnp.int32, (8, LANES), 0)
    row3 = sub - 3 * (sub // 3)
    row = lax.broadcasted_iota(jnp.int32, (8, width), 0)
    lane = lax.broadcasted_iota(jnp.int32, (8, width), 1)
    pos_x = moved(src_ref, task, pose_of(ids_ref[0, task]), row3, width)
    pos_y = moved(tgt_ref, task, pose_of(ids_ref[1, task]), row3, width)
    sq_x = pos_x * pos_x
    norm_x = pltpu.roll(sq_x, 1, 0) + pltpu.roll(sq_x, 2, 0) + pltpu.roll(sq_x, 3, 0)
    base_x = jnp.where(row < 6, pos_x, jnp.where(row == 6, LIFT - SPREAD * LOG2E * norm_x, 1.0))
    sq_y = pos_y * pos_y
    norm_y = pltpu.roll(sq_y, 2, 0) + pltpu.roll(sq_y, 3, 0) + pltpu.roll(sq_y, 4, 0)
    last_y = jnp.where(lane < counts_ref[1, task], -SPREAD * LOG2E * norm_y, FLOOR)
    base_y = jnp.where(row < 6, SCALE * pos_y, jnp.where(row == 6, 1.0, last_y))
    x_one, x_two, x_three = halves(base_x)
    y_one, y_two, y_three = halves(base_y)
    low3 = row < 3
    mid3 = (row >= 3) & (row < 6)
    x_group = [
        x_one,
        jnp.where(low3 | (row == 7), x_one, x_three),
        jnp.where(row == 7, x_one, x_two),
    ]
    y_group = [
        jnp.where(mid3, y_two, y_one),
        jnp.where(low3 | (row == 7), y_three, y_one),
        jnp.where(low3 | (row == 6), y_one, y_two),
    ]
    blank = jnp.zeros((8, width), jnp.float32)
    mat_x = jnp.concatenate(x_group + [blank], axis=0).astype(jnp.bfloat16)
    mat_y = jnp.concatenate(y_group + [blank], axis=0).astype(jnp.bfloat16)
    return pos_x, mat_x, mat_y


def score_of(turned_y, mat_x):
    return jnp.dot(turned_y, mat_x, preferred_element_type=jnp.float32)


def pull_sums(mat_y, weight):
    return jnp.dot(mat_y, weight.astype(jnp.bfloat16), preferred_element_type=jnp.float32)


def moments(task, live, counts_ref, pos_x, sums, acc_ref, low_ref):
    width = pos_x.shape[1]
    row = lax.broadcasted_iota(jnp.int32, (8, width), 0)
    lane = lax.broadcasted_iota(jnp.int32, (8, width), 1)
    count_x = jnp.where(task < live, counts_ref[0, task], 0)
    top = sums[:8]
    bottom = sums[8:]
    total = top[6:7, :]
    valid = lane < count_x
    low3 = row < 3
    low_ref[...] = jnp.minimum(low_ref[...], jnp.where(valid[:1], total, 1.0))
    inverse = jnp.broadcast_to((1.0 / SCALE) / total, (8, width))
    match_mid = (top + bottom + pltpu.roll(bottom, 3, 0)) * inverse
    match = jnp.where(valid, jnp.where(low3, pltpu.roll(match_mid, 5, 0), match_mid), 0.0)
    pos = jnp.where(valid, pos_x, 0.0)
    diff = pos - match
    next_pos = pltpu.roll(pos, 7, 0)
    ones = jnp.where(valid & (row == 6), 1.0, 0.0)
    linear = jnp.where(low3, pos, jnp.where(row < 6, match, ones))
    turned = jnp.where(low3, next_pos, pltpu.roll(match, 2, 0))
    cross = pos * pltpu.roll(diff, 7, 0) - next_pos * diff
    tail = jnp.where(low3, cross, diff)
    acc_lane = lax.broadcasted_iota(jnp.int32, (8, LANES), 1)
    for slot, part in enumerate((linear, linear * linear, linear * turned, tail)):
        reduced = jnp.sum(part, axis=1, keepdims=True)
        span = pl.ds(8 * slot, 8)
        acc_ref[span, :] = jnp.where(acc_lane == task, reduced, acc_ref[span, :])


def all_tasks(pose_of, data, work):
    live_ref, ids_ref, counts_ref, src_ref, tgt_ref = data
    acc_ref, low_ref, pos_ref, mx_ref, my_ref, mt_ref, sums_ref, even_ref, odd_ref, items_ref = work
    tasks = src_ref.shape[1]
    width = src_ref.shape[2]
    chunks = width // LANES
    live = live_ref[0]
    acc_ref[...] = jnp.zeros_like(acc_ref)
    low_ref[...] = jnp.ones_like(low_ref)
    mx_ref[tasks] = jnp.zeros_like(mx_ref[tasks])
    for chunk in range(chunks):
        my_ref[tasks * chunks + chunk] = jnp.zeros_like(my_ref[0])
        mt_ref[tasks * chunks + chunk] = jnp.zeros_like(mt_ref[0])
    unroll = UNROLL if tasks % UNROLL == 0 else 1
    groups = (live + unroll - 1) // unroll
    def prepare(group, end):
        for inner in range(unroll):
            task = group * unroll + inner
            pos_x, mat_x, mat_y = operands(task, pose_of, ids_ref, counts_ref, src_ref, tgt_ref)
            pos_ref[task] = pos_x
            mx_ref[task] = mat_x
            for chunk in range(chunks):
                block = mat_y[:, chunk * LANES : (chunk + 1) * LANES]
                my_ref[task * chunks + chunk] = block[:16]
                mt_ref[task * chunks + chunk] = block.T
            for chunk in range(chunks):
                items_ref[end + chunk] = task * chunks + chunk
            used = (counts_ref[1, task] + LANES - 1) // LANES
            end = end + jnp.where(task < live, used, 0)
        return end

    count = lax.fori_loop(0, groups, prepare, jnp.int32(0))
    for pad in range(3 * STEP):
        items_ref[count + pad] = tasks * chunks
    rounds = (count + STEP - 1) // STEP

    def score(index, buffer_ref, slot):
        code = items_ref[index]
        score = score_of(mt_ref[code], mx_ref[code // chunks])
        buffer_ref[slot] = jnp.exp2(score).astype(jnp.bfloat16)

    def pull(index, buffer_ref, slot):
        code = items_ref[index]
        task = code // chunks
        out = pull_sums(my_ref[code], buffer_ref[slot])
        prior = jnp.where(code == task * chunks, 0.0, sums_ref[task])
        sums_ref[task] = prior + out

    def both(group, next_ref, this_ref):
        for slot in range(STEP):
            score((group + 1) * STEP + slot, next_ref, slot)
            pull(group * STEP + slot, this_ref, slot)

    for slot in range(STEP):
        score(slot, even_ref, slot)

    def pair(index, carry):
        both(2 * index, odd_ref, even_ref)

        @pl.when(2 * index + 1 < rounds)
        def _():
            both(2 * index + 1, even_ref, odd_ref)

        return carry

    lax.fori_loop(0, (rounds + 1) // 2, pair, 0)

    def finish(group, carry):
        for inner in range(unroll):
            task = group * unroll + inner
            moments(task, live, counts_ref, pos_ref[task], sums_ref[task], acc_ref, low_ref)
        return carry

    lax.fori_loop(0, groups, finish, 0)

    @pl.when(jnp.min(low_ref[...]) < TINY)
    def _():
        def again(task, carry):
            pos_x, mat_x, mat_y = operands(task, pose_of, ids_ref, counts_ref, src_ref, tgt_ref)
            score = score_of(mat_y.T, mat_x)
            weight = jnp.exp2(score - jnp.max(score, axis=0, keepdims=True))
            moments(task, live, counts_ref, pos_x, pull_sums(mat_y[:16], weight), acc_ref, low_ref)
            return carry

        lax.fori_loop(0, live, again, 0)


def scatter(acc_ref, pairs_ref, scans):
    row_id = lax.broadcasted_iota(jnp.int32, (scans, LANES), 0)
    parts = jnp.concatenate(halves(acc_ref[...]), axis=0).astype(jnp.bfloat16)

    def side(index):
        hot = (pairs_ref[index : index + 1, :] == row_id).astype(jnp.float32).astype(jnp.bfloat16)
        out = lax.dot_general(
            parts, hot, (((1,), (1,)), ((), ())), preferred_element_type=jnp.float32
        )
        return out[:32] + (out[32:64] + out[64:])

    sum_a = side(0)
    sum_b = side(1)
    row = lax.broadcasted_iota(jnp.int32, (8, scans), 0)

    def low(slot):
        span = slice(8 * slot, 8 * slot + 8)
        return sum_a[span] + pltpu.roll(sum_b[span], 5, 0)

    count = sum_a[:8] + sum_b[:8]
    mixed = low(2)
    tail = sum_a[24:] - sum_b[24:]
    first = jnp.where(row < 3, low(0), pltpu.roll(low(1), 3, 0))
    first = jnp.where(row < 6, first, jnp.where(row == 6, count, pltpu.roll(mixed, 7, 0)))
    second = jnp.where(row < 6, tail, pltpu.roll(mixed, 5, 0))
    return first, second


def updated(first, second, pose_rows, fixed):
    def cross(a, b):
        return (
            a[1] * b[2] - a[2] * b[1],
            a[2] * b[0] - a[0] * b[2],
            a[0] * b[1] - a[1] * b[0],
        )

    at = lambda arr, index: arr[index : index + 1, :]
    lin = [at(first, k) for k in range(3)]
    xx, yy, zz = (at(first, 3 + k) for k in range(3))
    mass = at(first, 6) + DAMPING
    xy = at(first, 7)
    yz = at(second, 6)
    zx = at(second, 7)
    turn = [at(second, 1), at(second, 2), at(second, 0)]
    pull = [at(second, 3 + k) for k in range(3)]
    inverse = 1.0 / mass
    sx, sy, sz = lin
    ux, uy, uz = sx * inverse, sy * inverse, sz * inverse
    h00 = (yy + zz) + DAMPING - (sy * uy + sz * uz)
    h11 = (xx + zz) + DAMPING - (sx * ux + sz * uz)
    h22 = (xx + yy) + DAMPING - (sx * ux + sy * uy)
    h01 = sx * uy - xy
    h02 = sx * uz - zx
    h12 = sy * uz - yz
    lever = cross((ux, uy, uz), pull)
    r0, r1, r2 = (lever[k] - turn[k] for k in range(3))
    i0 = 1.0 / h00
    l1 = h01 * i0
    l2 = h02 * i0
    d1 = h11 - l1 * h01
    e12 = h12 - l1 * h02
    d2 = h22 - l2 * h02
    y1 = r1 - l1 * r0
    y2 = r2 - l2 * r0
    i1 = 1.0 / d1
    m12 = e12 * i1
    w2 = (y2 - m12 * y1) / (d2 - m12 * e12)
    w1 = y1 * i1 - m12 * w2
    w0 = r0 * i0 - l1 * w1 - l2 * w2
    swing = cross(lin, (w0, w1, w2))
    shift = [jnp.where(fixed, 0.0, (swing[k] - pull[k]) * inverse) for k in range(3)]
    cx, cy, cz = (jnp.where(fixed, 0.0, 0.5 * w) for w in (w0, w1, w2))
    norm = cx * cx + cy * cy + cz * cz
    gain = 2.0 / (1.0 + norm)
    step = [
        [1.0 + gain * (cx * cx - norm), gain * (cx * cy - cz), gain * (cx * cz + cy)],
        [gain * (cx * cy + cz), 1.0 + gain * (cy * cy - norm), gain * (cy * cz - cx)],
        [gain * (cx * cz - cy), gain * (cy * cz + cx), 1.0 + gain * (cz * cz - norm)],
    ]
    out = []
    for i in range(3):
        for j in range(3):
            out.append(sum(step[i][k] * pose_rows[3 * k + j] for k in range(3)))
    for i in range(3):
        out.append(sum(step[i][k] * pose_rows[9 + k] for k in range(3)) + shift[i])
    return out


def send(out_ref, acc_ref, pairs_ref):
    first, second = scatter(acc_ref, pairs_ref, out_ref.shape[2])
    for home in range(out_ref.shape[0]):
        out_ref[home, :8, :] = first
        out_ref[home, 8:, :] = second


def first_kernel(live_ref, ids_ref, counts_ref, pose_ref, src_ref, tgt_ref, pairs_ref, out_ref, *work):
    scan_dev = out_ref.shape[2] // out_ref.shape[0]
    pitch = pose_ref.shape[0] // out_ref.shape[0]

    def pose_of(scan):
        home = lax.div(scan, jnp.int32(scan_dev))
        base = home * pitch + (scan - home * scan_dev) * 12
        return lambda k, r: pose_ref[base + (9 + r if k == 3 else 3 * r + k)]

    all_tasks(pose_of, (live_ref, ids_ref, counts_ref, src_ref, tgt_ref), work)
    send(out_ref, work[0], pairs_ref)


def receive(in_ref):
    first = in_ref[0, :8, :]
    second = in_ref[0, 8:, :]
    for home in range(1, in_ref.shape[0]):
        first = first + in_ref[home, :8, :]
        second = second + in_ref[home, 8:, :]
    return first, second


def new_poses(in_ref, rows_ref, gauge_ref):
    first, second = receive(in_ref)
    scans = in_ref.shape[2]
    fixed = lax.broadcasted_iota(jnp.int32, (1, scans), 1) == gauge_ref[0]
    return updated(first, second, [rows_ref[k : k + 1, :] for k in range(12)], fixed)


def second_kernel(live_ref, ids_ref, counts_ref, gauge_ref, in_ref, rows_ref, src_ref, tgt_ref, pairs_ref, out_ref, next_ref, *work):
    table_ref, sem = work[-2:]
    for k, new_row in enumerate(new_poses(in_ref, rows_ref, gauge_ref)):
        next_ref[k : k + 1, :] = new_row
    copy = pltpu.make_async_copy(next_ref, table_ref, sem)
    copy.start()
    copy.wait()

    def pose_of(scan):
        return lambda k, r: table_ref[9 + r if k == 3 else 3 * r + k, scan]

    all_tasks(pose_of, (live_ref, ids_ref, counts_ref, src_ref, tgt_ref), work[:-2])
    send(out_ref, work[0], pairs_ref)


def last_kernel(own_ref, gauge_ref, in_ref, rows_ref, out_ref):
    scans = in_ref.shape[2]
    rows = new_poses(in_ref, rows_ref, gauge_ref)
    block = jnp.concatenate(rows + [jnp.zeros((LANES - 12, scans), jnp.float32)], axis=0)
    block = pltpu.roll(block, scans - own_ref[0], 1)[:, :LANES]
    out_ref[...] = block.T[: out_ref.shape[0], :12]


def body(source_points, target_points, pair_scans, point_counts, live_tasks, pose_init, gauge):
    homes = lax.axis_size(AXES)
    scan_dev = pose_init.shape[0]
    scans = homes * scan_dev
    tasks, _, width = source_points.shape
    chunks = width // LANES
    smem = pl.BlockSpec(memory_space=pltpu.SMEM)
    vmem = pl.BlockSpec(memory_space=pltpu.VMEM)
    scratch = [
        pltpu.VMEM((32, LANES), jnp.float32),
        pltpu.VMEM((1, width), jnp.float32),
        pltpu.VMEM((tasks, 8, width), jnp.float32),
        pltpu.VMEM((tasks + 1, 32, width), jnp.bfloat16),
        pltpu.VMEM(((tasks + 1) * chunks, 16, LANES), jnp.bfloat16),
        pltpu.VMEM(((tasks + 1) * chunks, LANES, 32), jnp.bfloat16),
        pltpu.VMEM((tasks + 1, 16, width), jnp.float32),
        pltpu.VMEM((STEP, LANES, width), jnp.bfloat16),
        pltpu.VMEM((STEP, LANES, width), jnp.bfloat16),
        pltpu.SMEM((tasks * chunks + 4 * STEP,), jnp.int32),
    ]
    parts = jax.ShapeDtypeStruct((homes, 16, scans), jnp.float32)
    rows_shape = jax.ShapeDtypeStruct((12, scans), jnp.float32)
    swap = lambda value: lax.all_to_all(value, AXES, 0, 0, tiled=True)

    source = jnp.transpose(source_points, (1, 0, 2))
    target = jnp.transpose(target_points, (1, 0, 2))
    ids = pair_scans.T
    counts = point_counts.T
    pairs = jnp.pad(ids, ((0, 0), (0, LANES - tasks)), constant_values=-1)
    own = (lax.axis_index(AXES) * scan_dev).reshape(1).astype(jnp.int32)

    flat = scan_dev * 12
    pitch = -(-flat // LANES) * LANES
    mine = jnp.pad(pose_init.reshape(1, flat), ((0, 0), (0, pitch - flat)))
    poses = swap(jnp.broadcast_to(mine, (homes, pitch)))
    rows = poses[:, :flat].reshape(scans, 12).T
    sums = pl.pallas_call(
        first_kernel,
        out_shape=parts,
        in_specs=[smem] * 4 + [vmem] * 3,
        out_specs=vmem,
        scratch_shapes=scratch,
        name="terms_first",
    )(live_tasks, ids, counts, poses.reshape(-1), source, target, pairs)
    sums, rows = pl.pallas_call(
        second_kernel,
        out_shape=(parts, rows_shape),
        in_specs=[smem] * 4 + [vmem] * 5,
        out_specs=(vmem, vmem),
        scratch_shapes=scratch + [pltpu.SMEM((12, scans), jnp.float32), pltpu.SemaphoreType.DMA],
        name="terms_second",
    )(live_tasks, ids, counts, gauge, swap(sums), rows, source, target, pairs)
    return pl.pallas_call(
        last_kernel,
        out_shape=jax.ShapeDtypeStruct((scan_dev, 12), jnp.float32),
        in_specs=[smem] * 2 + [vmem] * 2,
        out_specs=vmem,
        name="update_last",
    )(own, gauge, swap(sums), rows)


def solution(mesh):
    spec = P(AXES, None)
    cube = P(AXES, None, None)
    return jax.shard_map(
        body,
        mesh=mesh,
        in_specs=(cube, cube, spec, spec, P(AXES), spec, P()),
        out_specs=spec,
        check_vma=False,
    )
```

profile of v0, /device:TPU:0, one launch (start us, length us, event | category | flops | bytes accessed | tf_op | source)
XLA Modules:
  0.0 102.3 jit_solution(17551035785126958630)
XLA Ops:
  0.0 0.8 reshape.20
  0.8 0.6 broadcast_in_dim.2
  1.4 7.3 %all-to-all-start = ((f32[32,1,128]{2,1,0:T(1,128)}), f32[32,1,128]{2,1,0:T(1,128)S(1)}, u32[]{:S(2)}, u32[]{:S(2)}) async-start(f32[32,1,128]{2,1,0:T(1,128)} %broadcast_in_dim.2), calls=%async_computation | async-start | bytes 32768 | tf_op jit(solution)/shard_map/all_to_all | solution.py:372
  9.4 0.0 copy-start.4
  9.4 0.7 copy-done.4
  10.0 0.6 pad.12.pairs_ref
  10.6 5.3 %all-to-all-done = f32[32,1,128]{2,1,0:T(1,128)S(1)} async-done(((f32[32,1,128]{2,1,0:T(1,128)}), f32[32,1,128]{2,1,0:T(1,128)S(1)}, u32[]{:S(2)}, u32[]{:S(2)}) %all-to-all-start) | async-done | bytes 16416 | tf_op jit(solution)/shard_map/all_to_all | solution.py:372
  15.9 0.0 copy-start.2
  15.9 0.6 copy-done.2
  16.5 9.4 %terms_first.1 = f32[32,16,128]{2,1,0:T(8,128)} custom-call(s32[1]{0:T(128)S(6)} %copy.10.live_ref, s32[2,32]{1,0:T(2,128)} %bitcast.18, s32[2,32]{1,0:T(2,128)} %bitcast.21, f32[4096]{0:T(1024)} %bitcast.15, f32[3,32,384]{2,1,0:T(8,128)} %bitcast.11, f32[3,32,384]{2,1,0:T(8,128)} %bitcast.13, s32[2,128]{1,0:T(2,128)} %pad.12.pairs_ref), custom_call_target="tpu_custom_call" | custom-call | tf_op jit(solution)/shard_map/terms_first/pallas_call | solution.py:386
  25.9 0.0 copy-start.3
  25.9 20.8 %all-to-all-start.1 = ((f32[32,16,128]{2,1,0:T(8,128)}), f32[32,16,128]{2,1,0:T(8,128)S(1)}, u32[]{:S(2)}, u32[]{:S(2)}) async-start(f32[32,16,128]{2,1,0:T(8,128)} %terms_first.1), calls=%async_computation.1 | async-start | bytes 524288 | tf_op jit(solution)/shard_map/all_to_all | solution.py:372
  47.3 0.0 copy-done.3
  47.3 0.1 reshape.22
  47.4 0.7 copy.9
  48.1 8.8 %all-to-all-done.1.in_ref = f32[32,16,128]{2,1,0:T(8,128)S(1)} async-done(((f32[32,16,128]{2,1,0:T(8,128)}), f32[32,16,128]{2,1,0:T(8,128)S(1)}, u32[]{:S(2)}, u32[]{:S(2)}) %all-to-all-start.1) | async-done | bytes 262176 | tf_op jit(solution)/shard_map/all_to_all | solution.py:372
  56.9 0.0 copy-start.1
  56.9 0.7 copy-done.1
  57.6 10.2 %terms_second.1 = (f32[32,16,128]{2,1,0:T(8,128)}, f32[12,128]{1,0:T(8,128)}) custom-call(s32[1]{0:T(128)S(6)} %copy.10.live_ref, s32[2,32]{1,0:T(2,128)} %bitcast.19, s32[2,32]{1,0:T(2,128)} %bitcast.22, s32[1]{0:T(128)S(6)} %copy.11.gauge_ref, f32[32,16,128]{2,1,0:T(8,128)} %copy-done.1, f32[12,128]{1,0:T(8,128)} %bitcast.17, f32[3,32,384]{2,1,0:T(8,128)} %bitcast.12, ...), custom_call_target="tpu_custom_call" | custom-call | tf_op jit(solution)/shard_map/terms_second/pallas_call | solution.py:394
  67.8 21.8 %all-to-all-start.2 = ((f32[32,16,128]{2,1,0:T(8,128)}), f32[32,16,128]{2,1,0:T(8,128)S(1)}, u32[]{:S(2)}, u32[]{:S(2)}) async-start(f32[32,16,128]{2,1,0:T(8,128)} %get-tuple-element.7), calls=%async_computation.2 | async-start | bytes 524288 | tf_op jit(solution)/shard_map/all_to_all | solution.py:372
  89.6 10.2 %all-to-all-done.2.in_ref = f32[32,16,128]{2,1,0:T(8,128)S(1)} async-done(((f32[32,16,128]{2,1,0:T(8,128)}), f32[32,16,128]{2,1,0:T(8,128)S(1)}, u32[]{:S(2)}, u32[]{:S(2)}) %all-to-all-start.2) | async-done | bytes 262176 | tf_op jit(solution)/shard_map/all_to_all | solution.py:372
  99.9 0.0 copy-start
  99.9 0.7 copy-done
  100.6 1.8 %update_last.1 = f32[4,12]{1,0:T(4,128)} custom-call(s32[1]{0:T(128)} %bitcast.own_ref, s32[1]{0:T(128)S(6)} %copy.11.gauge_ref, f32[32,16,128]{2,1,0:T(8,128)} %copy-done, f32[12,128]{1,0:T(8,128)} %get-tuple-element.8.rows_ref), custom_call_target="tpu_custom_call" | custom-call | tf_op jit(solution)/shard_map/update_last/pallas_call | solution.py:402
  (1 shorter events, 0.0 us)
Async XLA Ops:
  1.4 14.5 %all-to-all-start = ((f32[32,1,128]{2,1,0:T(1,128)}), f32[32,1,128]{2,1,0:T(1,128)S(1)}, u32[]{:S(2)}, u32[]{:S(2)}) async-start(f32[32,1,128]{2,1,0:T(1,128)} %broadcast_in_dim.2), calls=%async_computation | async-start | bytes 32768 | tf_op jit(solution)/shard_map/all_to_all | solution.py:372
  9.4 0.7 copy-start.4
  15.9 0.6 copy-start.2
  25.9 21.4 %copy-start.3 = (f32[32,1,128]{2,1,0:T(1,128)S(1)}, f32[32,1,128]{2,1,0:T(1,128)}, u32[]{:S(2)}) copy-start(f32[32,1,128]{2,1,0:T(1,128)} %copy-done.2) | copy-start | bytes 49156
  25.9 31.0 %all-to-all-start.1 = ((f32[32,16,128]{2,1,0:T(8,128)}), f32[32,16,128]{2,1,0:T(8,128)S(1)}, u32[]{:S(2)}, u32[]{:S(2)}) async-start(f32[32,16,128]{2,1,0:T(8,128)} %terms_first.1), calls=%async_computation.1 | async-start | bytes 524288 | tf_op jit(solution)/shard_map/all_to_all | solution.py:372
  56.9 0.7 copy-start.1
  67.8 32.1 %all-to-all-start.2 = ((f32[32,16,128]{2,1,0:T(8,128)}), f32[32,16,128]{2,1,0:T(8,128)S(1)}, u32[]{:S(2)}, u32[]{:S(2)}) async-start(f32[32,16,128]{2,1,0:T(8,128)} %get-tuple-element.7), calls=%async_computation.2 | async-start | bytes 524288 | tf_op jit(solution)/shard_map/all_to_all | solution.py:372
  99.9 0.7 copy-start
where the time goes:
time: 101 us; the launch traced here: 102 us
  starting transfers between devices  49.9 us (49%)
  waiting for transfers between devices  24.4 us (24%)
  Pallas kernels  21.3 us (21%)
  local copies, waits for them, and re-layouts  5.38 us (5%)
  between operations  1.36 us (1%)
    all_to_all x3, starting transfers between devices, body(): swap = lambda value: lax.all_to_all(value, AXES, 0, 0, tiled=True)  49.9 us
    all_to_all x3, waiting for transfers between devices, body(): swap = lambda value: lax.all_to_all(value, AXES, 0, 0, tiled=True)  24.4 us
    pallas_call x1, Pallas kernels, body(): pl.pallas_call(second_kernel, out_shape=(parts, rows_shape), in_specs=[sm...  10.2 us
    pallas_call x1, Pallas kernels, body(): pl.pallas_call(first_kernel, out_shape=parts, in_specs=[smem] * 4 + [vmem...  9.4 us
    unnamed x10, local copies, waits for them, and re-layouts  2.68 us
  transfers between devices with their start and end apart: 3, of which 3 were waited for; matrix products, arithmetic and copies ran while one was open for 1% of the time, Pallas kernels for 0%

commit v1 on v0

--- a/solution.py
+++ b/solution.py
@@ -17,6 +17,7 @@
 STEP = 8
 SCALE = 2.0 * SPREAD * LOG2E
 LANES = 128
+INNER_LIMIT = 1 << 20
 
 
 def halves(value):
@@ -325,7 +326,10 @@
 
 
 def second_kernel(live_ref, ids_ref, counts_ref, gauge_ref, in_ref, rows_ref, src_ref, tgt_ref, pairs_ref, out_ref, next_ref, *work):
-    table_ref, sem = work[-2:]
+    turn_ref, table_ref, sem = work[-3:]
+    scans = in_ref.shape[2]
+    homes = out_ref.shape[0]
+    scan_dev = scans // homes
     for k, new_row in enumerate(new_poses(in_ref, rows_ref, gauge_ref)):
         next_ref[k : k + 1, :] = new_row
     copy = pltpu.make_async_copy(next_ref, table_ref, sem)
@@ -335,16 +339,34 @@
     def pose_of(scan):
         return lambda k, r: table_ref[9 + r if k == 3 else 3 * r + k, scan]
 
-    all_tasks(pose_of, (live_ref, ids_ref, counts_ref, src_ref, tgt_ref), work[:-2])
-    send(out_ref, work[0], pairs_ref)
+    all_tasks(pose_of, (live_ref, ids_ref, counts_ref, src_ref, tgt_ref), work[:-3])
+    first, second = scatter(work[0], pairs_ref, scans)
+    blank = jnp.zeros((LANES - 16, scans), jnp.float32)
+    turn_ref[...] = jnp.concatenate([first, second, blank], axis=0).T
+    out = turn_ref[pl.ds(0, homes, stride=scan_dev), :]
+    for local in range(1, scan_dev):
+        out = out + pltpu.roll(turn_ref[pl.ds(local, homes, stride=scan_dev), :], 16 * local, 1)
+    out_ref[...] = out
 
 
 def last_kernel(own_ref, gauge_ref, in_ref, rows_ref, out_ref):
-    scans = in_ref.shape[2]
-    rows = new_poses(in_ref, rows_ref, gauge_ref)
-    block = jnp.concatenate(rows + [jnp.zeros((LANES - 12, scans), jnp.float32)], axis=0)
-    block = pltpu.roll(block, scans - own_ref[0], 1)[:, :LANES]
-    out_ref[...] = block.T[: out_ref.shape[0], :12]
+    scan_dev = out_ref.shape[0]
+    scans = rows_ref.shape[1]
+    blank = jnp.zeros((4, scans), jnp.float32)
+    rows = jnp.concatenate([rows_ref[...], blank], axis=0)
+    rows = pltpu.roll(rows, scans - own_ref[0], 1)[:, :LANES]
+    total = jnp.sum(in_ref[...], axis=0, keepdims=True)
+    turned = jnp.broadcast_to(total, (LANES, LANES)).T
+    lane = lax.broadcasted_iota(jnp.int32, (8, LANES), 1)
+    first = turned[:8]
+    second = turned[8:16]
+    for local in range(1, scan_dev):
+        first = jnp.where(lane == local, turned[16 * local : 16 * local + 8], first)
+        second = jnp.where(lane == local, turned[16 * local + 8 : 16 * local + 16], second)
+    fixed = lane[:1] + own_ref[0] == gauge_ref[0]
+    new = updated(first, second, [rows[k : k + 1] for k in range(12)], fixed)
+    block = jnp.concatenate(new + [jnp.zeros((LANES - 12, LANES), jnp.float32)], axis=0)
+    out_ref[...] = block.T[:scan_dev, :12]
 
 
 def body(source_points, target_points, pair_scans, point_counts, live_tasks, pose_init, gauge):
@@ -368,19 +390,26 @@
         pltpu.SMEM((tasks * chunks + 4 * STEP,), jnp.int32),
     ]
     parts = jax.ShapeDtypeStruct((homes, 16, scans), jnp.float32)
+    blocks = jax.ShapeDtypeStruct((homes, LANES), jnp.float32)
     rows_shape = jax.ShapeDtypeStruct((12, scans), jnp.float32)
     swap = lambda value: lax.all_to_all(value, AXES, 0, 0, tiled=True)
 
-    source = jnp.transpose(source_points, (1, 0, 2))
-    target = jnp.transpose(target_points, (1, 0, 2))
     ids = pair_scans.T
     counts = point_counts.T
-    pairs = jnp.pad(ids, ((0, 0), (0, LANES - tasks)), constant_values=-1)
     own = (lax.axis_index(AXES) * scan_dev).reshape(1).astype(jnp.int32)
+
+
+    def inner(value):
+        if value.size > INNER_LIMIT:
+            return value
+        return pltpu.with_memory_space_constraint(value, pltpu.VMEM)
 
     flat = scan_dev * 12
     pitch = -(-flat // LANES) * LANES
     mine = jnp.pad(pose_init.reshape(1, flat), ((0, 0), (0, pitch - flat)))
+    source = jnp.transpose(source_points, (1, 0, 2))
+    target = jnp.transpose(target_points, (1, 0, 2))
+    pairs = inner(jnp.pad(ids, ((0, 0), (0, LANES - tasks)), constant_values=-1))
     poses = swap(jnp.broadcast_to(mine, (homes, pitch)))
     rows = poses[:, :flat].reshape(scans, 12).T
     sums = pl.pallas_call(
@@ -393,19 +422,24 @@
     )(live_tasks, ids, counts, poses.reshape(-1), source, target, pairs)
     sums, rows = pl.pallas_call(
         second_kernel,
-        out_shape=(parts, rows_shape),
+        out_shape=(blocks, rows_shape),
         in_specs=[smem] * 4 + [vmem] * 5,
         out_specs=(vmem, vmem),
-        scratch_shapes=scratch + [pltpu.SMEM((12, scans), jnp.float32), pltpu.SemaphoreType.DMA],
+        scratch_shapes=scratch
+        + [
+            pltpu.VMEM((scans, LANES), jnp.float32),
+            pltpu.SMEM((12, scans), jnp.float32),
+            pltpu.SemaphoreType.DMA,
+        ],
         name="terms_second",
-    )(live_tasks, ids, counts, gauge, swap(sums), rows, source, target, pairs)
+    )(live_tasks, ids, counts, gauge, inner(swap(sums)), inner(rows), source, target, pairs)
     return pl.pallas_call(
         last_kernel,
         out_shape=jax.ShapeDtypeStruct((scan_dev, 12), jnp.float32),
         in_specs=[smem] * 2 + [vmem] * 2,
         out_specs=vmem,
         name="update_last",
-    )(own, gauge, swap(sums), rows)
+    )(own, gauge, inner(swap(sums)), inner(rows))
 
 
 def solution(mesh):

time: 101 us -> 95.6 us (0.947); the launches traced: 102 us -> 94.1 us
  starting transfers between devices: 49.9 us -> 40.2 us
  Pallas kernels: 21.3 us -> 27.3 us
  local copies, waits for them, and re-layouts: 5.38 us -> 2.81 us
  waiting for transfers between devices: 24.4 us -> 22.5 us
    all_to_all x3, starting transfers between devices: 49.9 us -> 40.2 us  [body(): swap = lambda value: lax.all_to_all(value, AXES, 0, 0, tiled=True)]
    pallas_call x1, Pallas kernels: 10.2 us -> 13.7 us  [body(): pl.pallas_call(second_kernel, out_shape=(blocks, rows_shape), in_specs=[s...]
    pallas_call x1, Pallas kernels: 9.4 us -> 12.8 us  [body(): pl.pallas_call(first_kernel, out_shape=parts, in_specs=[smem] * 4 + [vmem...]
    all_to_all x3, waiting for transfers between devices: 24.4 us -> 22.5 us  [body(): swap = lambda value: lax.all_to_all(value, AXES, 0, 0, tiled=True)]
    unnamed x10 -> x8, local copies, waits for them, and re-layouts: 2.68 us -> 1.28 us
  transfers between devices with their start and end apart: 3 -> 3, of which waited for: 3 -> 3; matrix products, arithmetic and copies ran while one was open for 1% -> 0% of each run, Pallas kernels for 0% -> 0%
where the time goes in v1:
time: 95.6 us; the launch traced here: 94.1 us
  starting transfers between devices  40.2 us (42%)
  Pallas kernels  27.3 us (29%)
  waiting for transfers between devices  22.5 us (24%)
  local copies, waits for them, and re-layouts  2.81 us (3%)
  between operations  1.37 us (1%)
    all_to_all x3, starting transfers between devices, body(): swap = lambda value: lax.all_to_all(value, AXES, 0, 0, tiled=True)  40.2 us
    all_to_all x3, waiting for transfers between devices, body(): swap = lambda value: lax.all_to_all(value, AXES, 0, 0, tiled=True)  22.5 us
    pallas_call x1, Pallas kernels, body(): pl.pallas_call(second_kernel, out_shape=(blocks, rows_shape), in_specs=[s...  13.7 us
    pallas_call x1, Pallas kernels, body(): pl.pallas_call(first_kernel, out_shape=parts, in_specs=[smem] * 4 + [vmem...  12.8 us
  transfers between devices with their start and end apart: 3, of which 3 were waited for; matrix products, arithmetic and copies ran while one was open for 0% of the time, Pallas kernels for 0%

profile of v1, /device:TPU:0, one launch (start us, length us, event | category | flops | bytes accessed | tf_op | source)
XLA Modules:
  0.0 94.1 jit_solution(4322973273056658803)
XLA Ops:
  0.0 0.8 reshape.22
  0.8 0.6 broadcast_in_dim.2
  1.4 7.3 %all-to-all-start = ((f32[32,1,128]{2,1,0:T(1,128)}), f32[32,1,128]{2,1,0:T(1,128)S(1)}, u32[]{:S(2)}, u32[]{:S(2)}) async-start(f32[32,1,128]{2,1,0:T(1,128)} %broadcast_in_dim.2), calls=%async_computation | async-start | bytes 32768 | tf_op jit(solution)/shard_map/all_to_all | solution.py:395
  9.4 0.0 copy-start.3
  9.4 0.7 copy-done.3
  10.1 5.8 %all-to-all-done = f32[32,1,128]{2,1,0:T(1,128)S(1)} async-done(((f32[32,1,128]{2,1,0:T(1,128)}), f32[32,1,128]{2,1,0:T(1,128)S(1)}, u32[]{:S(2)}, u32[]{:S(2)}) %all-to-all-start) | async-done | bytes 16416 | tf_op jit(solution)/shard_map/all_to_all | solution.py:395
  15.9 0.0 copy-start.1
  15.9 0.6 copy-done.1
  16.5 12.8 %terms_first.1 = f32[32,16,128]{2,1,0:T(8,128)} custom-call(s32[1]{0:T(128)S(6)} %copy.11.live_ref, s32[2,32]{1,0:T(2,128)} %bitcast.24, s32[2,32]{1,0:T(2,128)} %bitcast.27, f32[4096]{0:T(1024)} %bitcast.21, f32[3,32,384]{2,1,0:T(8,128)} %bitcast.17, f32[3,32,384]{2,1,0:T(8,128)} %bitcast.19, s32[2,128]{1,0:T(2,128)S(1)} %pad.12.pairs_ref), custom_call_target="tpu_custom_call" | custom-call | tf_op jit(solution)/shard_map/terms_first/pallas_call | solution.py:415
  29.3 0.0 copy-start.2
  29.3 16.3 %all-to-all-start.1 = ((f32[32,16,128]{2,1,0:T(8,128)}), f32[32,16,128]{2,1,0:T(8,128)S(1)}, u32[]{:S(2)}, u32[]{:S(2)}) async-start(f32[32,16,128]{2,1,0:T(8,128)} %terms_first.1), calls=%async_computation.1 | async-start | bytes 524288 | tf_op jit(solution)/shard_map/all_to_all | solution.py:395
  46.2 0.0 copy-done.2
  46.2 0.1 reshape.24
  46.3 0.1 copy.9
  46.4 9.5 %all-to-all-done.1.in_ref = f32[32,16,128]{2,1,0:T(8,128)S(1)} async-done(((f32[32,16,128]{2,1,0:T(8,128)}), f32[32,16,128]{2,1,0:T(8,128)S(1)}, u32[]{:S(2)}, u32[]{:S(2)}) %all-to-all-start.1) | async-done | bytes 262176 | tf_op jit(solution)/shard_map/all_to_all | solution.py:395
  55.8 13.7 %terms_second.1 = (f32[32,128]{1,0:T(8,128)}, f32[12,128]{1,0:T(8,128)}) custom-call(s32[1]{0:T(128)S(6)} %copy.11.live_ref, s32[2,32]{1,0:T(2,128)} %bitcast.25, s32[2,32]{1,0:T(2,128)} %bitcast.28, s32[1]{0:T(128)S(6)} %copy.12.gauge_ref, f32[32,16,128]{2,1,0:T(8,128)S(1)} %all-to-all-done.1.in_ref, f32[12,128]{1,0:T(8,128)S(1)} %bitcast.16, ...), custom_call_target="tpu_custom_call" | custom-call | tf_op jit(solution)/shard_map/terms_second/pallas_call | solution.py:423
  69.5 16.6 %all-to-all-start.2 = ((f32[32,1,128]{2,1,0:T(1,128)}), f32[32,1,128]{2,1,0:T(1,128)S(1)}, u32[]{:S(2)}, u32[]{:S(2)}) async-start(f32[32,1,128]{2,1,0:T(1,128)} %bitcast.23), calls=%async_computation.2 | async-start | bytes 32768 | tf_op jit(solution)/shard_map/all_to_all | solution.py:395
  86.1 0.0 copy-start
  86.1 7.2 %all-to-all-done.2 = f32[32,1,128]{2,1,0:T(1,128)S(1)} async-done(((f32[32,1,128]{2,1,0:T(1,128)}), f32[32,1,128]{2,1,0:T(1,128)S(1)}, u32[]{:S(2)}, u32[]{:S(2)}) %all-to-all-start.2) | async-done | bytes 16416 | tf_op jit(solution)/shard_map/all_to_all | solution.py:395
  93.3 0.0 copy-done
  93.3 0.8 update_last.1
  (2 shorter events, 0.0 us)
Async XLA Ops:
  1.4 14.5 %all-to-all-start = ((f32[32,1,128]{2,1,0:T(1,128)}), f32[32,1,128]{2,1,0:T(1,128)S(1)}, u32[]{:S(2)}, u32[]{:S(2)}) async-start(f32[32,1,128]{2,1,0:T(1,128)} %broadcast_in_dim.2), calls=%async_computation | async-start | bytes 32768 | tf_op jit(solution)/shard_map/all_to_all | solution.py:395
  9.4 0.7 copy-start.3
  15.9 0.6 copy-start.1
  29.3 16.9 %copy-start.2 = (f32[32,1,128]{2,1,0:T(1,128)S(1)}, f32[32,1,128]{2,1,0:T(1,128)}, u32[]{:S(2)}) copy-start(f32[32,1,128]{2,1,0:T(1,128)} %copy-done.1) | copy-start | bytes 49156
  29.3 26.5 %all-to-all-start.1 = ((f32[32,16,128]{2,1,0:T(8,128)}), f32[32,16,128]{2,1,0:T(8,128)S(1)}, u32[]{:S(2)}, u32[]{:S(2)}) async-start(f32[32,16,128]{2,1,0:T(8,128)} %terms_first.1), calls=%async_computation.1 | async-start | bytes 524288 | tf_op jit(solution)/shard_map/all_to_all | solution.py:395
  69.5 23.8 %all-to-all-start.2 = ((f32[32,1,128]{2,1,0:T(1,128)}), f32[32,1,128]{2,1,0:T(1,128)S(1)}, u32[]{:S(2)}, u32[]{:S(2)}) async-start(f32[32,1,128]{2,1,0:T(1,128)} %bitcast.23), calls=%async_computation.2 | async-start | bytes 32768 | tf_op jit(solution)/shard_map/all_to_all | solution.py:395
  86.1 7.2 %copy-start = (f32[12,128]{1,0:T(8,128)S(1)}, f32[12,128]{1,0:T(8,128)}, u32[]{:S(2)}) copy-start(f32[12,128]{1,0:T(8,128)} %get-tuple-element.8.rows_ref) | copy-start | bytes 18436

commit v2 on v1

v2 whole, which is shorter than its diff:
```python
import functools

import jax
import jax.numpy as jnp
from jax import lax
from jax.experimental import pallas as pl
from jax.experimental.pallas import tpu as pltpu
from jax.sharding import PartitionSpec as P

AXES = ("gx", "gy", "gz")
ITERS = 2
SPREAD = 2.0
DAMPING = 1.0
FLOOR = -1e30
LOG2E = 1.4426950408889634
LIFT = 100.0
TINY = 2.0**-100
ROWS = 24
STEP = 8
SCALE = 2.0 * SPREAD * LOG2E
LANES = 128
INNER_LIMIT = 1 << 20


def halves(value):
    first = value.astype(jnp.bfloat16).astype(jnp.float32)
    rest = value - first
    second = rest.astype(jnp.bfloat16).astype(jnp.float32)
    return first, second, rest - second


def score_of(turned_y, mat_x):
    return jnp.dot(turned_y, mat_x, preferred_element_type=jnp.float32)


def gather_columns(gathered, live, meta_ref, cols_ref):
    lane = lax.broadcasted_iota(jnp.int32, (1, LANES), 1)
    meta = meta_ref[...]
    count_x = jnp.where(lane < live, meta[2:3], 0).astype(jnp.float32)
    count_y = meta[3:4].astype(jnp.float32)
    ids = meta[:2].astype(jnp.float32)
    blank = jnp.zeros((LANES - 36, LANES), jnp.float32)
    parts = [gathered[:, :LANES], gathered[:, LANES:], count_x, count_y, ids, blank]
    cols_ref[...] = jnp.concatenate(parts, axis=0).T


def one_hot(values, rows):
    row = lax.broadcasted_iota(jnp.int32, (rows, values.shape[1]), 0)
    return jnp.where(row == values, 1.0, 0.0).astype(jnp.bfloat16)


def both_ids(meta_ref):
    meta = meta_ref[...]
    return jnp.concatenate([meta[0:1], meta[1:2]], axis=1)


def all_tasks(live_ref, counts_ref, src_ref, tgt_ref, work):
    cols_ref, vals_ref, low_ref, pos_ref, fx_ref, fy_ref, sums_ref = work[:7]
    even_ref, odd_ref, turn_even_ref, turn_odd_ref, items_ref, owner_ref = work[7:]
    tasks = src_ref.shape[1]
    width = src_ref.shape[2]
    chunks = width // LANES
    slots = tasks + 1
    live = live_ref[0]
    groups = (live + 7) // 8
    vals_ref[...] = jnp.zeros_like(vals_ref)
    low_ref[...] = jnp.ones_like(low_ref)
    for chunk in range(chunks):
        dead = pl.ds((chunk * slots + tasks) * ROWS, ROWS)
        fx_ref[dead, :] = jnp.zeros((ROWS, LANES), jnp.float32)
        fy_ref[dead, :] = jnp.zeros((ROWS, LANES), jnp.float32)
    lane_wide = lax.broadcasted_iota(jnp.int32, (8, width), 1).astype(jnp.float32)

    def prepare(group, end):
        base = pl.multiple_of(group * 8, 8)
        cols = cols_ref[pl.ds(base, 8), :]

        def place(points_ref, offset):
            raw = [points_ref[axis, pl.ds(base, 8), :] for axis in range(3)]
            out = []
            for r in range(3):
                value = cols[:, offset + 9 + r : offset + 10 + r]
                for axis in range(3):
                    entry = offset + 3 * r + axis
                    value = value + cols[:, entry : entry + 1] * raw[axis]
                out.append(value)
            return out, out[0] * out[0] + out[1] * out[1] + out[2] * out[2]

        pos, norm_x = place(src_ref, 0)
        for axis in range(3):
            pos_ref[axis, pl.ds(base, 8), :] = pos[axis]
        x_parts = [halves(value) for value in pos]
        n_parts = halves(LIFT - SPREAD * LOG2E * norm_x)
        pos_y, norm_y = place(tgt_ref, 16)
        inside = lane_wide < cols[:, 33:34]
        y_parts = [halves(SCALE * value) for value in pos_y]
        m_parts = halves(jnp.where(inside, -SPREAD * LOG2E * norm_y, FLOOR))
        one = jnp.ones((8, width), jnp.float32)
        pairs = []
        for first, second in ((0, 0), (0, 1), (0, 2)):
            pairs += [(x_parts[k][first], y_parts[k][second]) for k in range(3)]
        pairs += [(n_parts[k], one) for k in range(3)]
        pairs += [(x_parts[k][1], y_parts[k][0]) for k in range(3)]
        pairs += [(one, m_parts[0])]
        pairs += [(x_parts[k][1], y_parts[k][1]) for k in range(3)]
        pairs += [(x_parts[k][2], y_parts[k][0]) for k in range(3)]
        pairs += [(one, m_parts[1]), (one, m_parts[2])]
        for r, (left, right) in enumerate(pairs):
            for chunk in range(chunks):
                span = slice(chunk * LANES, (chunk + 1) * LANES)
                rows = pl.ds((chunk * slots + base) * ROWS + r, 8, stride=ROWS)
                fx_ref[rows, :] = left[:, span]
                fy_ref[rows, :] = right[:, span]
        for inner in range(8):
            task = jnp.minimum(base + inner, tasks - 1)
            for chunk in range(chunks):
                items_ref[end + chunk] = chunk * slots + task
                owner_ref[end + chunk] = task
            used = (counts_ref[1, task] + LANES - 1) // LANES
            end = end + jnp.where(base + inner < live, used, 0)
        return end

    for pad in range(STEP):
        items_ref[pad] = tasks
        owner_ref[pad] = tasks
    end = lax.fori_loop(0, groups, prepare, jnp.int32(STEP))

    def fill(pad, carry):
        items_ref[end + pad] = tasks
        owner_ref[end + pad] = tasks
        return carry

    lax.fori_loop(0, 3 * STEP, fill, 0)
    rounds = (end - 1) // STEP
    blank_x = jnp.zeros((32 - ROWS, width), jnp.float32)
    blank_y = jnp.zeros((32 - ROWS, LANES), jnp.float32)

    def factor_x(task):
        parts = [fx_ref[pl.ds((chunk * slots + task) * ROWS, ROWS), :] for chunk in range(chunks)]
        whole = jnp.concatenate([jnp.concatenate(parts, axis=1), blank_x], axis=0)
        return whole.astype(jnp.bfloat16)

    def turn_y(code):
        part = fy_ref[pl.ds(code * ROWS, ROWS), :]
        return jnp.concatenate([part, blank_y], axis=0).astype(jnp.bfloat16).T

    def pull_sums(code, weight):
        part = fy_ref[pl.ds(code * ROWS, 16), :].astype(jnp.bfloat16)
        return jnp.dot(part, weight, preferred_element_type=jnp.float32)

    def add_sums(task, out, first):
        for chunk in range(chunks):
            rows = pl.ds((chunk * slots + task) * 16, 16)
            part = out[:, chunk * LANES : (chunk + 1) * LANES]
            sums_ref[rows, :] = part + jnp.where(first, 0.0, sums_ref[rows, :])

    def turn(index, turned_ref, slot):
        turned_ref[slot] = turn_y(items_ref[index])

    def score(index, turned_ref, buffer_ref, slot):
        value = score_of(turned_ref[slot], factor_x(owner_ref[index]))
        buffer_ref[slot] = jnp.exp2(value).astype(jnp.bfloat16)

    def pull(index, buffer_ref, slot):
        code = items_ref[index]
        add_sums(owner_ref[index], pull_sums(code, buffer_ref[slot]), code <= tasks)

    def all_stages(group, this_ref, next_ref, turn_this_ref, turn_next_ref):
        for slot in range(STEP):
            score((group + 1) * STEP + slot, turn_next_ref, next_ref, slot)
            pull(group * STEP + slot, this_ref, slot)
            turn((group + 2) * STEP + slot, turn_this_ref, slot)

    for slot in range(STEP):
        turn(STEP + slot, turn_odd_ref, slot)

    def pair(index, carry):
        all_stages(2 * index, even_ref, odd_ref, turn_even_ref, turn_odd_ref)

        @pl.when(2 * index < rounds)
        def _():
            all_stages(2 * index + 1, odd_ref, even_ref, turn_odd_ref, turn_even_ref)

        return carry

    lax.fori_loop(0, rounds // 2 + 1, pair, 0)

    def finish(group):
        base = pl.multiple_of(group * 8, 8)
        cols = cols_ref[pl.ds(base, 8), :]
        lane = lax.broadcasted_iota(jnp.int32, (8, LANES), 1)
        totals = None
        for chunk in range(chunks):
            span = slice(chunk * LANES, (chunk + 1) * LANES)

            def row(index):
                rows = pl.ds((chunk * slots + base) * 16 + index, 8, stride=16)
                return sums_ref[rows, :]

            valid = lane_wide[:, span] < cols[:, 32:33]
            weight = row(9)
            low_ref[...] = jnp.minimum(low_ref[...], jnp.where(valid, weight, 1.0))
            inverse = (1.0 / SCALE) / weight
            match = []
            for k in range(3):
                value = (row(k) + row(3 + k) + row(6 + k)) * inverse
                match.append(jnp.where(valid, value, 0.0))
            pos = [jnp.where(valid, pos_ref[k, pl.ds(base, 8), span], 0.0) for k in range(3)]
            diff = [pos[k] - match[k] for k in range(3)]

            def shape(p):
                return [p[0], p[1], p[2], p[0] * p[0], p[1] * p[1], p[2] * p[2]]

            def mixed(p):
                return [p[0] * p[1], p[1] * p[2], p[2] * p[0]]

            values = shape(pos) + [jnp.where(valid, 1.0, 0.0)] + mixed(pos)[:1]
            values += list(cross(pos, diff)) + diff + mixed(pos)[1:]
            values += shape(match) + mixed(match)
            totals = values if totals is None else [p + q for p, q in zip(totals, values)]
        sums = [jnp.sum(value, axis=1, keepdims=True) for value in totals]
        order = sums[:16] + sums[16:22] + [sums[6], sums[22]]
        order += [-value for value in sums[8:14]] + sums[23:25]
        out = jnp.zeros((8, LANES), jnp.float32)
        for index, value in enumerate(order):
            out = jnp.where(lane == index, value, out)
        vals_ref[pl.ds(base, 8), :] = out

    def finish_all():
        def step(index, carry):
            for inner in range(wide):
                finish(index * wide + inner)
            return carry

        wide = 2 if tasks % 16 == 0 else 1
        lax.fori_loop(0, (groups + wide - 1) // wide, step, 0)

    finish_all()

    @pl.when(jnp.min(low_ref[...]) < TINY)
    def _():
        def again(task, carry):
            mat_x = factor_x(task)
            scores = [score_of(turn_y(chunk * slots + task), mat_x) for chunk in range(chunks)]
            top = jnp.max(scores[0], axis=0, keepdims=True)
            for value in scores[1:]:
                top = jnp.maximum(top, jnp.max(value, axis=0, keepdims=True))
            for chunk in range(chunks):
                weight = jnp.exp2(scores[chunk] - top).astype(jnp.bfloat16)
                add_sums(task, pull_sums(chunk * slots + task, weight), chunk == 0)
            return carry

        lax.fori_loop(0, live, again, 0)
        finish_all()


def pack(vals_ref, cols_ref, first_scan, tasks, scan_dev):
    sub = lax.broadcasted_iota(jnp.int32, (8, LANES), 0)
    lane = lax.broadcasted_iota(jnp.int32, (8, LANES), 1)
    tile = jnp.zeros((8, LANES), jnp.float32)
    own = [None] * scan_dev
    for group in range(tasks // 8):
        vals = vals_ref[8 * group : 8 * group + 8, :]
        cols = cols_ref[8 * group : 8 * group + 8, :]
        begin = 16 * group
        moved = pltpu.roll(vals, (begin - 16) % LANES, 1)
        tile = jnp.where((lane >= begin) & (lane < begin + 16), moved, tile)
        tile = jnp.where(lane == 80 + group, pltpu.roll(cols, 45 + group, 1), tile)
        for local in range(scan_dev):
            here = cols[:, 34:35] == (first_scan + local).astype(jnp.float32)
            part = jnp.where(here, vals, 0.0)
            own[local] = part if own[local] is None else own[local] + part
    sums = jnp.zeros((8, LANES), jnp.float32)
    for local in range(scan_dev):
        sums = jnp.where(sub == local, jnp.sum(own[local], axis=0, keepdims=True), sums)
    return jnp.where((lane >= 64) & (lane < 80), pltpu.roll(sums, 64, 1), tile)


def unpack(tiles, scans, groups, scan_dev):
    depth = tiles.shape[0]
    ids = tiles.T[80:88]
    spot = lax.broadcasted_iota(jnp.int32, (1, depth), 1)
    local = spot - 8 * (spot // 8)
    own = jnp.where(local < scan_dev, (spot // 8) * scan_dev + local, -1).astype(jnp.float32)
    row = lax.broadcasted_iota(jnp.int32, (scans, depth), 0).astype(jnp.float32)
    rows = [ids[group : group + 1] for group in range(groups)] + [own]
    hot = jnp.concatenate([jnp.where(row == ids_row, 1.0, 0.0) for ids_row in rows], axis=0)
    parts = jnp.concatenate(halves(tiles), axis=1).astype(jnp.bfloat16)
    out = jnp.dot(hot.astype(jnp.bfloat16), parts, preferred_element_type=jnp.float32)
    out = out[:, :LANES] + (out[:, LANES : 2 * LANES] + out[:, 2 * LANES :])
    total = out[:scans]
    for index in range(1, groups + 1):
        begin = 64 if index == groups else 16 * index
        total = total + pltpu.roll(out[index * scans : (index + 1) * scans], LANES - begin, 1)
    total = total.T
    return total[:8], total[8:16]


def scatter(vals_ref, hot_ref):
    vals = vals_ref[...]
    lane = lax.broadcasted_iota(jnp.int32, (LANES, LANES), 1)
    near = jnp.where(lane < 16, vals, 0.0)
    far = jnp.where(lane < 16, pltpu.roll(vals, LANES - 16, 1), 0.0)
    parts = jnp.concatenate(halves(jnp.concatenate([near, far], axis=0)), axis=1)
    out = jnp.dot(hot_ref[...], parts.astype(jnp.bfloat16), preferred_element_type=jnp.float32)
    return out[:, :LANES] + (out[:, LANES : 2 * LANES] + out[:, 2 * LANES :])


def cross(a, b):
    return (
        a[1] * b[2] - a[2] * b[1],
        a[2] * b[0] - a[0] * b[2],
        a[0] * b[1] - a[1] * b[0],
    )


def updated(first, second, pose_rows, fixed):
    at = lambda arr, index: arr[index : index + 1, :]
    lin = [at(first, k) for k in range(3)]
    xx, yy, zz = (at(first, 3 + k) for k in range(3))
    mass = at(first, 6) + DAMPING
    xy = at(first, 7)
    yz = at(second, 6)
    zx = at(second, 7)
    turn = [at(second, k) for k in range(3)]
    pull = [at(second, 3 + k) for k in range(3)]
    inverse = 1.0 / mass
    sx, sy, sz = lin
    ux, uy, uz = sx * inverse, sy * inverse, sz * inverse
    h00 = (yy + zz) + DAMPING - (sy * uy + sz * uz)
    h11 = (xx + zz) + DAMPING - (sx * ux + sz * uz)
    h22 = (xx + yy) + DAMPING - (sx * ux + sy * uy)
    h01 = sx * uy - xy
    h02 = sx * uz - zx
    h12 = sy * uz - yz
    lever = cross((ux, uy, uz), pull)
    r0, r1, r2 = (lever[k] - turn[k] for k in range(3))
    i0 = 1.0 / h00
    l1 = h01 * i0
    l2 = h02 * i0
    d1 = h11 - l1 * h01
    e12 = h12 - l1 * h02
    d2 = h22 - l2 * h02
    y1 = r1 - l1 * r0
    y2 = r2 - l2 * r0
    i1 = 1.0 / d1
    m12 = e12 * i1
    w2 = (y2 - m12 * y1) / (d2 - m12 * e12)
    w1 = y1 * i1 - m12 * w2
    w0 = r0 * i0 - l1 * w1 - l2 * w2
    swing = cross(lin, (w0, w1, w2))
    shift = [jnp.where(fixed, 0.0, (swing[k] - pull[k]) * inverse) for k in range(3)]
    cx, cy, cz = (jnp.where(fixed, 0.0, 0.5 * w) for w in (w0, w1, w2))
    norm = cx * cx + cy * cy + cz * cz
    gain = 2.0 / (1.0 + norm)
    step = [
        [1.0 + gain * (cx * cx - norm), gain * (cx * cy - cz), gain * (cx * cz + cy)],
        [gain * (cx * cy + cz), 1.0 + gain * (cy * cy - norm), gain * (cy * cz - cx)],
        [gain * (cx * cz - cy), gain * (cy * cz + cx), 1.0 + gain * (cz * cz - norm)],
    ]
    out = []
    for i in range(3):
        for j in range(3):
            out.append(sum(step[i][k] * pose_rows[3 * k + j] for k in range(3)))
    for i in range(3):
        out.append(sum(step[i][k] * pose_rows[9 + k] for k in range(3)) + shift[i])
    return out


def first_kernel(live_ref, counts_ref, own_ref, pose_ref, meta_ref, src_ref, tgt_ref, out_ref, *refs, scan_dev):
    hot_ref, work = refs[0], refs[1:]
    homes = out_ref.shape[0]
    ids = both_ids(meta_ref)
    home = lax.div(ids, jnp.int32(scan_dev))
    parts = jnp.concatenate(halves(pose_ref[...]), axis=1).astype(jnp.bfloat16)
    wide = lax.dot_general(
        parts,
        one_hot(jnp.where(ids < 0, -1, home), homes),
        (((0,), (0,)), ((), ())),
        preferred_element_type=jnp.float32,
    )
    pitch = pose_ref.shape[1]
    wide = wide[:pitch] + (wide[pitch : 2 * pitch] + wide[2 * pitch :])
    gathered = wide[:16]
    for local in range(1, scan_dev):
        here = ids - home * scan_dev == local
        gathered = jnp.where(here, wide[16 * local : 16 * local + 16], gathered)
    gather_columns(gathered, live_ref[0], meta_ref, work[0])
    all_tasks(live_ref, counts_ref, src_ref, tgt_ref, work)
    if out_ref.shape[1] == 8:
        total = pack(work[1], work[0], own_ref[0], src_ref.shape[1], scan_dev)
    else:
        hot_ref[...] = one_hot(ids, out_ref.shape[2])
        total = scatter(work[1], hot_ref).T[:16]
    for index in range(homes):
        out_ref[index] = total


def receive(in_ref):
    first = in_ref[0, :8, :]
    second = in_ref[0, 8:, :]
    for home in range(1, in_ref.shape[0]):
        first = first + in_ref[home, :8, :]
        second = second + in_ref[home, 8:, :]
    return first, second


def second_kernel(live_ref, counts_ref, gauge_ref, meta_ref, in_ref, rows_ref, src_ref, tgt_ref, out_ref, next_ref, *refs):
    hot_ref, work, turn_ref = refs[0], refs[1:-1], refs[-1]
    scans = rows_ref.shape[1]
    homes = out_ref.shape[0]
    scan_dev = scans // homes
    hot_ref[...] = one_hot(both_ids(meta_ref), scans)
    fixed = lax.broadcasted_iota(jnp.int32, (1, scans), 1) == gauge_ref[0]
    rows = [rows_ref[k : k + 1, :] for k in range(12)]
    if len(in_ref.shape) == 2:
        totals = unpack(in_ref[...], scans, src_ref.shape[1] // 8, scan_dev)
    else:
        totals = receive(in_ref)
    rows = updated(*totals, rows, fixed) + [jnp.zeros((4, scans), jnp.float32)]
    table = jnp.concatenate(rows, axis=0)
    next_ref[...] = table
    parts = jnp.concatenate(halves(table), axis=0).astype(jnp.bfloat16)
    wide = jnp.dot(parts, hot_ref[...], preferred_element_type=jnp.float32)
    gathered = wide[:16] + (wide[16:32] + wide[32:])
    gather_columns(gathered, live_ref[0], meta_ref, work[0])
    all_tasks(live_ref, counts_ref, src_ref, tgt_ref, work)
    turn_ref[...] = scatter(work[1], hot_ref)
    out = turn_ref[pl.ds(0, homes, stride=scan_dev), :]
    for local in range(1, scan_dev):
        out = out + pltpu.roll(turn_ref[pl.ds(local, homes, stride=scan_dev), :], 16 * local, 1)
    out_ref[...] = out


def last_kernel(own_ref, gauge_ref, in_ref, rows_ref, out_ref):
    scan_dev = out_ref.shape[0]
    scans = rows_ref.shape[1]
    rows = pltpu.roll(rows_ref[...], scans - own_ref[0], 1)[:, :LANES]
    total = jnp.sum(in_ref[...], axis=0, keepdims=True)
    turned = jnp.broadcast_to(total, (LANES, LANES)).T
    lane = lax.broadcasted_iota(jnp.int32, (8, LANES), 1)
    first = turned[:8]
    second = turned[8:16]
    for local in range(1, scan_dev):
        first = jnp.where(lane == local, turned[16 * local : 16 * local + 8], first)
        second = jnp.where(lane == local, turned[16 * local + 8 : 16 * local + 16], second)
    fixed = lane[:1] + own_ref[0] == gauge_ref[0]
    new = updated(first, second, [rows[k : k + 1] for k in range(12)], fixed)
    block = jnp.concatenate(new + [jnp.zeros((LANES - 12, LANES), jnp.float32)], axis=0)
    out_ref[...] = block.T[:scan_dev, :12]


def body(source_points, target_points, pair_scans, point_counts, live_tasks, pose_init, gauge):
    homes = lax.axis_size(AXES)
    scan_dev = pose_init.shape[0]
    scans = homes * scan_dev
    tasks, _, width = source_points.shape
    chunks = width // LANES
    slots = tasks + 1
    smem = pl.BlockSpec(memory_space=pltpu.SMEM)
    vmem = pl.BlockSpec(memory_space=pltpu.VMEM)
    scratch = [
        pltpu.VMEM((scans, 2 * LANES), jnp.bfloat16),
        pltpu.VMEM((LANES, LANES), jnp.float32),
        pltpu.VMEM((LANES, LANES), jnp.float32),
        pltpu.VMEM((8, LANES), jnp.float32),
        pltpu.VMEM((3, tasks, width), jnp.float32),
        pltpu.VMEM((chunks * slots * ROWS, LANES), jnp.float32),
        pltpu.VMEM((chunks * slots * ROWS, LANES), jnp.float32),
        pltpu.VMEM((chunks * slots * 16, LANES), jnp.float32),
        pltpu.VMEM((STEP, LANES, width), jnp.bfloat16),
        pltpu.VMEM((STEP, LANES, width), jnp.bfloat16),
        pltpu.VMEM((STEP, LANES, 32), jnp.bfloat16),
        pltpu.VMEM((STEP, LANES, 32), jnp.bfloat16),
        pltpu.SMEM((tasks * chunks + 6 * STEP,), jnp.int32),
        pltpu.SMEM((tasks * chunks + 6 * STEP,), jnp.int32),
    ]
    swap = lambda value: lax.all_to_all(value, AXES, 0, 0, tiled=True)

    def inner(value):
        if value.size > INNER_LIMIT:
            return value
        return pltpu.with_memory_space_constraint(value, pltpu.VMEM)

    flat = scan_dev * 16
    pitch = -(-flat // LANES) * LANES
    mine = jnp.pad(pose_init, ((0, 0), (0, 4))).reshape(1, flat)
    mine = jnp.pad(mine, ((0, 0), (0, pitch - flat)))
    source = jnp.transpose(source_points, (1, 0, 2))
    target = jnp.transpose(target_points, (1, 0, 2))
    counts = point_counts.T
    meta = jnp.concatenate([pair_scans.T, counts], axis=0)
    meta = inner(jnp.pad(meta, ((0, 0), (0, LANES - tasks)), constant_values=-1))
    own = (lax.axis_index(AXES) * scan_dev).reshape(1).astype(jnp.int32)
    poses = swap(jnp.broadcast_to(mine, (homes, pitch)))
    rows = poses[:, :flat].reshape(scans, 16).T
    packed = tasks <= 32 and tasks % 8 == 0 and scan_dev <= 8 and homes <= 64
    shape = (homes, 8, LANES) if packed else (homes, 16, scans)
    sums = pl.pallas_call(
        functools.partial(first_kernel, scan_dev=scan_dev),
        out_shape=jax.ShapeDtypeStruct(shape, jnp.float32),
        in_specs=[smem] * 3 + [vmem] * 4,
        out_specs=vmem,
        scratch_shapes=scratch,
        name="terms_first",
    )(live_tasks, counts, own, inner(poses), meta, source, target)
    sums = swap(sums)
    if packed:
        sums = sums.reshape(homes * 8, LANES)
    sums, rows = pl.pallas_call(
        second_kernel,
        out_shape=(
            jax.ShapeDtypeStruct((homes, LANES), jnp.float32),
            jax.ShapeDtypeStruct((16, scans), jnp.float32),
        ),
        in_specs=[smem] * 3 + [vmem] * 5,
        out_specs=(vmem, vmem),
        scratch_shapes=scratch + [pltpu.VMEM((scans, LANES), jnp.float32)],
        name="terms_second",
    )(live_tasks, counts, gauge, meta, inner(sums), inner(rows), source, target)
    return pl.pallas_call(
        last_kernel,
        out_shape=jax.ShapeDtypeStruct((scan_dev, 12), jnp.float32),
        in_specs=[smem] * 2 + [vmem] * 2,
        out_specs=vmem,
        name="update_last",
    )(own, gauge, inner(swap(sums)), inner(rows))


def solution(mesh):
    spec = P(AXES, None)
    cube = P(AXES, None, None)
    return jax.shard_map(
        body,
        mesh=mesh,
        in_specs=(cube, cube, spec, spec, P(AXES), spec, P()),
        out_specs=spec,
        check_vma=False,
    )
```

time: 95.6 us -> 82.6 us (0.86); the launches traced: 94.1 us -> 82.2 us
  starting transfers between devices: 40.2 us -> 16.8 us
  blocking collectives: 0 us -> 16.8 us
  waiting for transfers between devices: 22.5 us -> 13.2 us
  Pallas kernels: 27.3 us -> 31.8 us
    all_to_all x3 -> x2, starting transfers between devices: 40.2 us -> 16.8 us  [body(): swap = lambda value: lax.all_to_all(value, AXES, 0, 0, tiled=True)]
    all_to_all x0 -> x1, blocking collectives: none -> 16.8 us  [body(): swap = lambda value: lax.all_to_all(value, AXES, 0, 0, tiled=True)]
    all_to_all x3 -> x2, waiting for transfers between devices: 22.5 us -> 13.2 us  [body(): swap = lambda value: lax.all_to_all(value, AXES, 0, 0, tiled=True)]
    pallas_call x2, Pallas kernels: 26.5 us -> 31 us  [the longest x1 15.8 us: body(): pl.pallas_call(second_kernel, out_shape=(jax.ShapeDtypeStruct((homes, LAN...]
  transfers between devices with their start and end apart: 3 -> 2, of which waited for: 3 -> 2; matrix products, arithmetic and copies ran while one was open for 0% -> 0% of each run, Pallas kernels for 0% -> 0%
where the time goes in v2:
time: 82.6 us; the launch traced here: 82.2 us
  Pallas kernels  31.8 us (38%)
  starting transfers between devices  16.8 us (20%)
  blocking collectives  16.8 us (20%)
  waiting for transfers between devices  13.2 us (16%)
  local copies, waits for them, and re-layouts  2.21 us (3%)
  between operations  1.35 us (2%)
    all_to_all x1, blocking collectives, body(): swap = lambda value: lax.all_to_all(value, AXES, 0, 0, tiled=True)  16.8 us
    all_to_all x2, starting transfers between devices, body(): swap = lambda value: lax.all_to_all(value, AXES, 0, 0, tiled=True)  16.8 us
    pallas_call x1, Pallas kernels, body(): pl.pallas_call(second_kernel, out_shape=(jax.ShapeDtypeStruct((homes, LAN...  15.8 us
    pallas_call x1, Pallas kernels, body(): pl.pallas_call(functools.partial(first_kernel, scan_dev=scan_dev), out_sh...  15.2 us
    all_to_all x2, waiting for transfers between devices, body(): swap = lambda value: lax.all_to_all(value, AXES, 0, 0, tiled=True)  13.2 us
  transfers between devices with their start and end apart: 2, of which 2 were waited for; matrix products, arithmetic and copies ran while one was open for 0% of the time, Pallas kernels for 0%

profile of v2, /device:TPU:0, one launch (start us, length us, event | category | flops | bytes accessed | tf_op | source)
XLA Modules:
  0.0 82.2 jit_solution(954888072814786562)
XLA Ops:
  0.0 0.7 pad.15
  0.7 0.1 reshape.21
  0.8 0.6 broadcast_in_dim.2
  1.4 7.3 %all-to-all-start = ((f32[32,1,128]{2,1,0:T(1,128)}), f32[32,1,128]{2,1,0:T(1,128)S(1)}, u32[]{:S(2)}, u32[]{:S(2)}) async-start(f32[32,1,128]{2,1,0:T(1,128)} %broadcast_in_dim.2), calls=%async_computation | async-start | bytes 32768 | tf_op jit(solution)/shard_map/all_to_all | solution.py:478
  8.7 0.0 copy-start.2
  8.7 0.0 copy-start.1
  8.7 0.7 copy-done.2
  9.4 0.0 copy-done.1
  10.1 5.8 %all-to-all-done = f32[32,1,128]{2,1,0:T(1,128)S(1)} async-done(((f32[32,1,128]{2,1,0:T(1,128)}), f32[32,1,128]{2,1,0:T(1,128)S(1)}, u32[]{:S(2)}, u32[]{:S(2)}) %all-to-all-start) | async-done | bytes 16416 | tf_op jit(solution)/shard_map/all_to_all | solution.py:478
  15.9 15.2 %terms_first.1 = f32[32,8,128]{2,1,0:T(8,128)} custom-call(s32[1]{0:T(128)S(6)} %copy.11.live_ref, s32[2,32]{1,0:T(2,128)} %bitcast.25, s32[1]{0:T(128)} %bitcast.own_ref, f32[32,128]{1,0:T(8,128)S(1)} %bitcast.16, s32[4,128]{1,0:T(4,128)S(1)} %pad.14.meta_ref, f32[3,32,384]{2,1,0:T(8,128)} %bitcast.20, f32[3,32,384]{2,1,0:T(8,128)} %bitcast.22), custom_call_target="tpu_custom_call" | custom-call | tf_op jit(solution)/shard_map/terms_first/pallas_call | solution.py:499
  31.1 9.5 %all-to-all-start.1 = ((f32[32,8,128]{2,1,0:T(8,128)}), f32[32,8,128]{2,1,0:T(8,128)S(1)}, u32[]{:S(2)}, u32[]{:S(2)}) async-start(f32[32,8,128]{2,1,0:T(8,128)} %terms_first.1), calls=%async_computation.1 | async-start | bytes 262144 | tf_op jit(solution)/shard_map/all_to_all | solution.py:478
  41.2 0.1 reshape.23
  41.3 0.1 copy.9
  41.4 7.4 %all-to-all-done.1 = f32[32,8,128]{2,1,0:T(8,128)S(1)} async-done(((f32[32,8,128]{2,1,0:T(8,128)}), f32[32,8,128]{2,1,0:T(8,128)S(1)}, u32[]{:S(2)}, u32[]{:S(2)}) %all-to-all-start.1) | async-done | bytes 131104 | tf_op jit(solution)/shard_map/all_to_all | solution.py:478
  48.8 15.8 %terms_second.1 = (f32[32,128]{1,0:T(8,128)}, f32[16,128]{1,0:T(8,128)}) custom-call(s32[1]{0:T(128)S(6)} %copy.11.live_ref, s32[2,32]{1,0:T(2,128)} %bitcast.26, s32[1]{0:T(128)S(6)} %copy.12.gauge_ref, s32[4,128]{1,0:T(4,128)S(1)} %pad.14.meta_ref, f32[256,128]{1,0:T(8,128)S(1)} %bitcast.15, f32[16,128]{1,0:T(8,128)S(1)} %bitcast.19, ...), custom_call_target="tpu_custom_call" | custom-call | tf_op jit(solution)/shard_map/terms_second/pallas_call | solution.py:510
  64.6 0.0 copy-start
  64.6 16.8 %all_to_all.24 = f32[32,1,128]{2,1,0:T(1,128)S(1)} all-to-all(f32[32,1,128]{2,1,0:T(1,128)} %bitcast.24), channel_id=1, replica_groups=mesh['gx'=2,'gy'=4,'gz'=4] {'gx','gy','gz'}, dimensions={0} | all-to-all | bytes 32768 | tf_op jit(solution)/shard_map/all_to_all | solution.py:478
  81.4 0.0 copy-done
  81.4 0.8 update_last.1
  (3 shorter events, 0.0 us)
Async XLA Ops:
  1.4 14.5 %all-to-all-start = ((f32[32,1,128]{2,1,0:T(1,128)}), f32[32,1,128]{2,1,0:T(1,128)S(1)}, u32[]{:S(2)}, u32[]{:S(2)}) async-start(f32[32,1,128]{2,1,0:T(1,128)} %broadcast_in_dim.2), calls=%async_computation | async-start | bytes 32768 | tf_op jit(solution)/shard_map/all_to_all | solution.py:478
  8.7 0.7 copy-start.2
  8.7 0.7 copy-start.1
  31.1 17.7 %all-to-all-start.1 = ((f32[32,8,128]{2,1,0:T(8,128)}), f32[32,8,128]{2,1,0:T(8,128)S(1)}, u32[]{:S(2)}, u32[]{:S(2)}) async-start(f32[32,8,128]{2,1,0:T(8,128)} %terms_first.1), calls=%async_computation.1 | async-start | bytes 262144 | tf_op jit(solution)/shard_map/all_to_all | solution.py:478
  64.6 16.8 %copy-start = (f32[16,128]{1,0:T(8,128)S(1)}, f32[16,128]{1,0:T(8,128)}, u32[]{:S(2)}) copy-start(f32[16,128]{1,0:T(8,128)} %get-tuple-element.8.rows_ref) | copy-start | bytes 24580

commit v3 on v2

--- a/solution.py
+++ b/solution.py
@@ -96,21 +96,20 @@
         y_parts = [halves(SCALE * value) for value in pos_y]
         m_parts = halves(jnp.where(inside, -SPREAD * LOG2E * norm_y, FLOOR))
         one = jnp.ones((8, width), jnp.float32)
-        pairs = []
-        for first, second in ((0, 0), (0, 1), (0, 2)):
-            pairs += [(x_parts[k][first], y_parts[k][second]) for k in range(3)]
-        pairs += [(n_parts[k], one) for k in range(3)]
-        pairs += [(x_parts[k][1], y_parts[k][0]) for k in range(3)]
-        pairs += [(one, m_parts[0])]
-        pairs += [(x_parts[k][1], y_parts[k][1]) for k in range(3)]
-        pairs += [(x_parts[k][2], y_parts[k][0]) for k in range(3)]
-        pairs += [(one, m_parts[1]), (one, m_parts[2])]
-        for r, (left, right) in enumerate(pairs):
-            for chunk in range(chunks):
-                span = slice(chunk * LANES, (chunk + 1) * LANES)
-                rows = pl.ds((chunk * slots + base) * ROWS + r, 8, stride=ROWS)
-                fx_ref[rows, :] = left[:, span]
-                fy_ref[rows, :] = right[:, span]
+        left = [part[0] for part in x_parts] + [part[1] for part in x_parts]
+        left += [n_parts[0], one] + [part[2] for part in x_parts]
+        left += [n_parts[1], n_parts[2], one, one, one]
+        right = [part[0] for part in y_parts] + [part[1] for part in y_parts]
+        right += [one, m_parts[0]] + [part[2] for part in y_parts]
+        right += [None, None, None, m_parts[2], m_parts[1]]
+        for ref, values in ((fx_ref, left), (fy_ref, right)):
+            for r, value in enumerate(values):
+                if value is None:
+                    continue
+                for chunk in range(chunks):
+                    span = slice(chunk * LANES, (chunk + 1) * LANES)
+                    rows = pl.ds((chunk * slots + base) * ROWS + r, 8, stride=ROWS)
+                    ref[rows, :] = value[:, span]
         for inner in range(8):
             task = jnp.minimum(base + inner, tasks - 1)
             for chunk in range(chunks):
@@ -123,7 +122,15 @@
     for pad in range(STEP):
         items_ref[pad] = tasks
         owner_ref[pad] = tasks
-    end = lax.fori_loop(0, groups, prepare, jnp.int32(STEP))
+    wide = 2 if tasks % 16 == 0 else 1
+
+    def prepare_some(index, end):
+        for inner in range(wide):
+            end = prepare(index * wide + inner, end)
+        return end
+
+    steps = (groups + wide - 1) // wide
+    end = lax.fori_loop(0, steps, prepare_some, jnp.int32(STEP))
 
     def fill(pad, carry):
         items_ref[end + pad] = tasks
@@ -132,17 +139,25 @@
 
     lax.fori_loop(0, 3 * STEP, fill, 0)
     rounds = (end - 1) // STEP
-    blank_x = jnp.zeros((32 - ROWS, width), jnp.float32)
-    blank_y = jnp.zeros((32 - ROWS, LANES), jnp.float32)
+    sub = lax.broadcasted_iota(jnp.int32, (8, LANES), 0)
 
     def factor_x(task):
-        parts = [fx_ref[pl.ds((chunk * slots + task) * ROWS, ROWS), :] for chunk in range(chunks)]
-        whole = jnp.concatenate([jnp.concatenate(parts, axis=1), blank_x], axis=0)
-        return whole.astype(jnp.bfloat16)
+        parts = [fx_ref[pl.ds((chunk * slots + task) * ROWS, 16), :] for chunk in range(chunks)]
+        whole = jnp.concatenate(parts, axis=1)
+        main, rest = whole[:8], whole[8:]
+        return jnp.concatenate([main, main, rest, main], axis=0).astype(jnp.bfloat16)
 
     def turn_y(code):
-        part = fy_ref[pl.ds(code * ROWS, ROWS), :]
-        return jnp.concatenate([part, blank_y], axis=0).astype(jnp.bfloat16).T
+        part = fy_ref[pl.ds(code * ROWS, 16), :]
+        main, rest = part[:8], part[8:]
+        last = jnp.where(sub == 7, rest, 0.0)
+        swapped = jnp.where(sub < 6, pltpu.roll(main, 3, 0), last)
+        swapped = jnp.where(sub < 3, pltpu.roll(main, 5, 0), swapped)
+        third = jnp.where(sub < 3, main, jnp.where(sub < 5, 1.0, 0.0))
+        last = jnp.where(sub == 7, pltpu.roll(rest, 1, 0), 0.0)
+        fourth = jnp.where(sub < 3, rest, last)
+        whole = jnp.concatenate([main, swapped, third, fourth], axis=0)
+        return whole.astype(jnp.bfloat16).T
 
     def pull_sums(code, weight):
         part = fy_ref[pl.ds(code * ROWS, 16), :].astype(jnp.bfloat16)
@@ -150,7 +165,7 @@
 
     def add_sums(task, out, first):
         for chunk in range(chunks):
-            rows = pl.ds((chunk * slots + task) * 16, 16)
+            rows = pl.ds((chunk * slots + task) * ROWS, 16)
             part = out[:, chunk * LANES : (chunk + 1) * LANES]
             sums_ref[rows, :] = part + jnp.where(first, 0.0, sums_ref[rows, :])
 
@@ -194,16 +209,16 @@
             span = slice(chunk * LANES, (chunk + 1) * LANES)
 
             def row(index):
-                rows = pl.ds((chunk * slots + base) * 16 + index, 8, stride=16)
+                rows = pl.ds((chunk * slots + base) * ROWS + index, 8, stride=ROWS)
                 return sums_ref[rows, :]
 
             valid = lane_wide[:, span] < cols[:, 32:33]
-            weight = row(9)
+            weight = row(6)
             low_ref[...] = jnp.minimum(low_ref[...], jnp.where(valid, weight, 1.0))
             inverse = (1.0 / SCALE) / weight
             match = []
             for k in range(3):
-                value = (row(k) + row(3 + k) + row(6 + k)) * inverse
+                value = (row(k) + row(3 + k) + row(8 + k)) * inverse
                 match.append(jnp.where(valid, value, 0.0))
             pos = [jnp.where(valid, pos_ref[k, pl.ds(base, 8), span], 0.0) for k in range(3)]
             diff = [pos[k] - match[k] for k in range(3)]
@@ -232,8 +247,7 @@
                 finish(index * wide + inner)
             return carry
 
-        wide = 2 if tasks % 16 == 0 else 1
-        lax.fori_loop(0, (groups + wide - 1) // wide, step, 0)
+        lax.fori_loop(0, steps, step, 0)
 
     finish_all()
 
@@ -467,7 +481,7 @@
         pltpu.VMEM((3, tasks, width), jnp.float32),
         pltpu.VMEM((chunks * slots * ROWS, LANES), jnp.float32),
         pltpu.VMEM((chunks * slots * ROWS, LANES), jnp.float32),
-        pltpu.VMEM((chunks * slots * 16, LANES), jnp.float32),
+        pltpu.VMEM((chunks * slots * ROWS, LANES), jnp.float32),
         pltpu.VMEM((STEP, LANES, width), jnp.bfloat16),
         pltpu.VMEM((STEP, LANES, width), jnp.bfloat16),
         pltpu.VMEM((STEP, LANES, 32), jnp.bfloat16),
@@ -490,6 +504,7 @@
     target = jnp.transpose(target_points, (1, 0, 2))
     counts = point_counts.T
     meta = jnp.concatenate([pair_scans.T, counts], axis=0)
+    counts = pltpu.with_memory_space_constraint(counts, pltpu.SMEM)
     meta = inner(jnp.pad(meta, ((0, 0), (0, LANES - tasks)), constant_values=-1))
     own = (lax.axis_index(AXES) * scan_dev).reshape(1).astype(jnp.int32)
     poses = swap(jnp.broadcast_to(mine, (homes, pitch)))

time: 82.6 us -> 81.4 us (0.985)
  Pallas kernels: 31.8 us -> 18 us
  blocking collectives: 16.8 us -> 23.3 us
  starting transfers between devices: 16.8 us -> 23 us
    pallas_call x1, Pallas kernels: 15.2 us -> 8.3 us  [body(): pl.pallas_call(functools.partial(first_kernel, scan_dev=scan_dev), out_sh...]
    pallas_call x1, Pallas kernels: 15.8 us -> 8.89 us  [body(): pl.pallas_call(second_kernel, out_shape=(jax.ShapeDtypeStruct((homes, LAN...]
    all_to_all x1, blocking collectives: 16.8 us -> 23.3 us  [body(): swap = lambda value: lax.all_to_all(value, AXES, 0, 0, tiled=True)]
    all_to_all x2, starting transfers between devices: 16.8 us -> 23 us  [body(): swap = lambda value: lax.all_to_all(value, AXES, 0, 0, tiled=True)]
where the time goes in v3:
time: 81.4 us; the launch traced here: 81.1 us
  blocking collectives  23.3 us (29%)
  starting transfers between devices  23 us (28%)
  Pallas kernels  18 us (22%)
  waiting for transfers between devices  13.2 us (16%)
  local copies, waits for them, and re-layouts  2.21 us (3%)
  between operations  1.35 us (2%)
    all_to_all x1, blocking collectives, body(): swap = lambda value: lax.all_to_all(value, AXES, 0, 0, tiled=True)  23.3 us
    all_to_all x2, starting transfers between devices, body(): swap = lambda value: lax.all_to_all(value, AXES, 0, 0, tiled=True)  23 us
    all_to_all x2, waiting for transfers between devices, body(): swap = lambda value: lax.all_to_all(value, AXES, 0, 0, tiled=True)  13.2 us
    pallas_call x1, Pallas kernels, body(): pl.pallas_call(second_kernel, out_shape=(jax.ShapeDtypeStruct((homes, LAN...  8.89 us
    pallas_call x1, Pallas kernels, body(): pl.pallas_call(functools.partial(first_kernel, scan_dev=scan_dev), out_sh...  8.3 us
  transfers between devices with their start and end apart: 2, of which 2 were waited for; matrix products, arithmetic and copies ran while one was open for 0% of the time, Pallas kernels for 0%

profile of v3, /device:TPU:0, one launch (start us, length us, event | category | flops | bytes accessed | tf_op | source)
XLA Modules:
  0.0 81.1 jit_solution(16721619241735242962)
XLA Ops:
  0.0 0.7 pad.15
  0.7 0.1 reshape.21
  0.8 0.6 broadcast_in_dim.2
  1.4 7.3 %all-to-all-start = ((f32[32,1,128]{2,1,0:T(1,128)}), f32[32,1,128]{2,1,0:T(1,128)S(1)}, u32[]{:S(2)}, u32[]{:S(2)}) async-start(f32[32,1,128]{2,1,0:T(1,128)} %broadcast_in_dim.2), calls=%async_computation | async-start | bytes 32768 | tf_op jit(solution)/shard_map/all_to_all | solution.py:492
  8.7 0.0 copy-start.2
  8.7 0.0 copy-start.1
  8.7 0.7 copy-done.2
  9.4 0.0 copy-done.1
  10.1 5.8 %all-to-all-done = f32[32,1,128]{2,1,0:T(1,128)S(1)} async-done(((f32[32,1,128]{2,1,0:T(1,128)}), f32[32,1,128]{2,1,0:T(1,128)S(1)}, u32[]{:S(2)}, u32[]{:S(2)}) %all-to-all-start) | async-done | bytes 16416 | tf_op jit(solution)/shard_map/all_to_all | solution.py:492
  15.9 8.3 %terms_first.1 = f32[32,8,128]{2,1,0:T(8,128)} custom-call(s32[1]{0:T(128)S(6)} %copy.11.live_ref, s32[2,32]{1,0:T(2,128)} %bitcast.25, s32[1]{0:T(128)} %bitcast.own_ref, f32[32,128]{1,0:T(8,128)S(1)} %bitcast.16, s32[4,128]{1,0:T(4,128)S(1)} %pad.14.meta_ref, f32[3,32,384]{2,1,0:T(8,128)} %bitcast.20, f32[3,32,384]{2,1,0:T(8,128)} %bitcast.22), custom_call_target="tpu_custom_call" | custom-call | tf_op jit(solution)/shard_map/terms_first/pallas_call | solution.py:514
  24.2 15.7 %all-to-all-start.1 = ((f32[32,8,128]{2,1,0:T(8,128)}), f32[32,8,128]{2,1,0:T(8,128)S(1)}, u32[]{:S(2)}, u32[]{:S(2)}) async-start(f32[32,8,128]{2,1,0:T(8,128)} %terms_first.1), calls=%async_computation.1 | async-start | bytes 262144 | tf_op jit(solution)/shard_map/all_to_all | solution.py:492
  40.5 0.1 reshape.23
  40.6 0.1 copy.9
  40.7 7.4 %all-to-all-done.1 = f32[32,8,128]{2,1,0:T(8,128)S(1)} async-done(((f32[32,8,128]{2,1,0:T(8,128)}), f32[32,8,128]{2,1,0:T(8,128)S(1)}, u32[]{:S(2)}, u32[]{:S(2)}) %all-to-all-start.1) | async-done | bytes 131104 | tf_op jit(solution)/shard_map/all_to_all | solution.py:492
  48.1 8.9 %terms_second.1 = (f32[32,128]{1,0:T(8,128)}, f32[16,128]{1,0:T(8,128)}) custom-call(s32[1]{0:T(128)S(6)} %copy.11.live_ref, s32[2,32]{1,0:T(2,128)} %bitcast.26, s32[1]{0:T(128)S(6)} %copy.12.gauge_ref, s32[4,128]{1,0:T(4,128)S(1)} %pad.14.meta_ref, f32[256,128]{1,0:T(8,128)S(1)} %bitcast.15, f32[16,128]{1,0:T(8,128)S(1)} %bitcast.19, ...), custom_call_target="tpu_custom_call" | custom-call | tf_op jit(solution)/shard_map/terms_second/pallas_call | solution.py:525
  57.0 0.0 copy-start
  57.0 23.3 %all_to_all.24 = f32[32,1,128]{2,1,0:T(1,128)S(1)} all-to-all(f32[32,1,128]{2,1,0:T(1,128)} %bitcast.24), channel_id=1, replica_groups=mesh['gx'=2,'gy'=4,'gz'=4] {'gx','gy','gz'}, dimensions={0} | all-to-all | bytes 32768 | tf_op jit(solution)/shard_map/all_to_all | solution.py:492
  80.2 0.0 copy-done
  80.2 0.8 %update_last.1 = f32[4,12]{1,0:T(4,128)} custom-call(s32[1]{0:T(128)} %bitcast.own_ref, s32[1]{0:T(128)S(6)} %copy.12.gauge_ref, f32[32,128]{1,0:T(8,128)S(1)} %bitcast.18, f32[16,128]{1,0:T(8,128)S(1)} %copy-done), custom_call_target="tpu_custom_call" | custom-call | tf_op jit(solution)/shard_map/update_last/pallas_call | solution.py:536
  (3 shorter events, 0.0 us)
Async XLA Ops:
  1.4 14.5 %all-to-all-start = ((f32[32,1,128]{2,1,0:T(1,128)}), f32[32,1,128]{2,1,0:T(1,128)S(1)}, u32[]{:S(2)}, u32[]{:S(2)}) async-start(f32[32,1,128]{2,1,0:T(1,128)} %broadcast_in_dim.2), calls=%async_computation | async-start | bytes 32768 | tf_op jit(solution)/shard_map/all_to_all | solution.py:492
  8.7 0.7 copy-start.2
  8.7 0.7 copy-start.1
  24.2 23.9 %all-to-all-start.1 = ((f32[32,8,128]{2,1,0:T(8,128)}), f32[32,8,128]{2,1,0:T(8,128)S(1)}, u32[]{:S(2)}, u32[]{:S(2)}) async-start(f32[32,8,128]{2,1,0:T(8,128)} %terms_first.1), calls=%async_computation.1 | async-start | bytes 262144 | tf_op jit(solution)/shard_map/all_to_all | solution.py:492
  57.0 23.3 %copy-start = (f32[16,128]{1,0:T(8,128)S(1)}, f32[16,128]{1,0:T(8,128)}, u32[]{:S(2)}) copy-start(f32[16,128]{1,0:T(8,128)} %get-tuple-element.8.rows_ref) | copy-start | bytes 24580

commit v4 on v3

--- a/solution.py
+++ b/solution.py
@@ -133,11 +133,12 @@
     end = lax.fori_loop(0, steps, prepare_some, jnp.int32(STEP))
 
     def fill(pad, carry):
-        items_ref[end + pad] = tasks
-        owner_ref[end + pad] = tasks
+        for inner in range(STEP):
+            items_ref[end + pad * STEP + inner] = tasks
+            owner_ref[end + pad * STEP + inner] = tasks
         return carry
 
-    lax.fori_loop(0, 3 * STEP, fill, 0)
+    lax.fori_loop(0, 3, fill, 0)
     rounds = (end - 1) // STEP
     sub = lax.broadcasted_iota(jnp.int32, (8, LANES), 0)
 
@@ -243,11 +244,12 @@
 
     def finish_all():
         def step(index, carry):
-            for inner in range(wide):
-                finish(index * wide + inner)
+            for inner in range(many):
+                finish(index * many + inner)
             return carry
 
-        lax.fori_loop(0, steps, step, 0)
+        many = 4 if tasks % 32 == 0 else wide
+        lax.fori_loop(0, (groups + many - 1) // many, step, 0)
 
     finish_all()
 

time: 81.4 us -> 82.3 us (1.011)
  Pallas kernels: 18 us -> 13.7 us
  starting transfers between devices: 23 us -> 25.9 us
  blocking collectives: 23.3 us -> 25.7 us
    all_to_all x2, starting transfers between devices: 23 us -> 25.9 us  [body(): swap = lambda value: lax.all_to_all(value, AXES, 0, 0, tiled=True)]
    all_to_all x1, blocking collectives: 23.3 us -> 25.7 us  [body(): swap = lambda value: lax.all_to_all(value, AXES, 0, 0, tiled=True)]
    pallas_call x1, Pallas kernels: 8.89 us -> 6.75 us  [body(): pl.pallas_call(second_kernel, out_shape=(jax.ShapeDtypeStruct((homes, LAN...]
    pallas_call x1, Pallas kernels: 8.3 us -> 6.16 us  [body(): pl.pallas_call(functools.partial(first_kernel, scan_dev=scan_dev), out_sh...]
where the time goes in v4:
time: 82.3 us; the launch traced here: 82.1 us
  starting transfers between devices  25.9 us (31%)
  blocking collectives  25.7 us (31%)
  Pallas kernels  13.7 us (17%)
  waiting for transfers between devices  13.2 us (16%)
  local copies, waits for them, and re-layouts  2.21 us (3%)
  between operations  1.35 us (2%)
    all_to_all x2, starting transfers between devices, body(): swap = lambda value: lax.all_to_all(value, AXES, 0, 0, tiled=True)  25.9 us
    all_to_all x1, blocking collectives, body(): swap = lambda value: lax.all_to_all(value, AXES, 0, 0, tiled=True)  25.7 us
    all_to_all x2, waiting for transfers between devices, body(): swap = lambda value: lax.all_to_all(value, AXES, 0, 0, tiled=True)  13.2 us
    pallas_call x1, Pallas kernels, body(): pl.pallas_call(second_kernel, out_shape=(jax.ShapeDtypeStruct((homes, LAN...  6.75 us
    pallas_call x1, Pallas kernels, body(): pl.pallas_call(functools.partial(first_kernel, scan_dev=scan_dev), out_sh...  6.16 us
  transfers between devices with their start and end apart: 2, of which 2 were waited for; matrix products, arithmetic and copies ran while one was open for 0% of the time, Pallas kernels for 0%

profile of v4, /device:TPU:0, one launch (start us, length us, event | category | flops | bytes accessed | tf_op | source)
XLA Modules:
  0.0 82.1 jit_solution(17732535648866253249)
XLA Ops:
  0.0 0.7 pad.15
  0.7 0.1 reshape.21
  0.8 0.6 broadcast_in_dim.2
  1.4 7.3 %all-to-all-start = ((f32[32,1,128]{2,1,0:T(1,128)}), f32[32,1,128]{2,1,0:T(1,128)S(1)}, u32[]{:S(2)}, u32[]{:S(2)}) async-start(f32[32,1,128]{2,1,0:T(1,128)} %broadcast_in_dim.2), calls=%async_computation | async-start | bytes 32768 | tf_op jit(solution)/shard_map/all_to_all | solution.py:494
  8.7 0.0 copy-start.2
  8.7 0.0 copy-start.1
  8.7 0.7 copy-done.2
  9.4 0.0 copy-done.1
  10.1 5.8 %all-to-all-done = f32[32,1,128]{2,1,0:T(1,128)S(1)} async-done(((f32[32,1,128]{2,1,0:T(1,128)}), f32[32,1,128]{2,1,0:T(1,128)S(1)}, u32[]{:S(2)}, u32[]{:S(2)}) %all-to-all-start) | async-done | bytes 16416 | tf_op jit(solution)/shard_map/all_to_all | solution.py:494
  15.9 6.2 %terms_first.1 = f32[32,8,128]{2,1,0:T(8,128)} custom-call(s32[1]{0:T(128)S(6)} %copy.11.live_ref, s32[2,32]{1,0:T(2,128)} %bitcast.25, s32[1]{0:T(128)} %bitcast.own_ref, f32[32,128]{1,0:T(8,128)S(1)} %bitcast.16, s32[4,128]{1,0:T(4,128)S(1)} %pad.14.meta_ref, f32[3,32,384]{2,1,0:T(8,128)} %bitcast.20, f32[3,32,384]{2,1,0:T(8,128)} %bitcast.22), custom_call_target="tpu_custom_call" | custom-call | tf_op jit(solution)/shard_map/terms_first/pallas_call | solution.py:516
  22.1 18.6 %all-to-all-start.1 = ((f32[32,8,128]{2,1,0:T(8,128)}), f32[32,8,128]{2,1,0:T(8,128)S(1)}, u32[]{:S(2)}, u32[]{:S(2)}) async-start(f32[32,8,128]{2,1,0:T(8,128)} %terms_first.1), calls=%async_computation.1 | async-start | bytes 262144 | tf_op jit(solution)/shard_map/all_to_all | solution.py:494
  41.3 0.1 reshape.23
  41.4 0.1 copy.9
  41.5 7.4 %all-to-all-done.1 = f32[32,8,128]{2,1,0:T(8,128)S(1)} async-done(((f32[32,8,128]{2,1,0:T(8,128)}), f32[32,8,128]{2,1,0:T(8,128)S(1)}, u32[]{:S(2)}, u32[]{:S(2)}) %all-to-all-start.1) | async-done | bytes 131104 | tf_op jit(solution)/shard_map/all_to_all | solution.py:494
  48.9 6.7 %terms_second.1 = (f32[32,128]{1,0:T(8,128)}, f32[16,128]{1,0:T(8,128)}) custom-call(s32[1]{0:T(128)S(6)} %copy.11.live_ref, s32[2,32]{1,0:T(2,128)} %bitcast.26, s32[1]{0:T(128)S(6)} %copy.12.gauge_ref, s32[4,128]{1,0:T(4,128)S(1)} %pad.14.meta_ref, f32[256,128]{1,0:T(8,128)S(1)} %bitcast.15, f32[16,128]{1,0:T(8,128)S(1)} %bitcast.19, ...), custom_call_target="tpu_custom_call" | custom-call | tf_op jit(solution)/shard_map/terms_second/pallas_call | solution.py:527
  55.6 0.0 copy-start
  55.6 25.7 %all_to_all.24 = f32[32,1,128]{2,1,0:T(1,128)S(1)} all-to-all(f32[32,1,128]{2,1,0:T(1,128)} %bitcast.24), channel_id=1, replica_groups=mesh['gx'=2,'gy'=4,'gz'=4] {'gx','gy','gz'}, dimensions={0} | all-to-all | bytes 32768 | tf_op jit(solution)/shard_map/all_to_all | solution.py:494
  81.3 0.0 copy-done
  81.3 0.8 update_last.1
  (3 shorter events, 0.0 us)
Async XLA Ops:
  1.4 14.5 %all-to-all-start = ((f32[32,1,128]{2,1,0:T(1,128)}), f32[32,1,128]{2,1,0:T(1,128)S(1)}, u32[]{:S(2)}, u32[]{:S(2)}) async-start(f32[32,1,128]{2,1,0:T(1,128)} %broadcast_in_dim.2), calls=%async_computation | async-start | bytes 32768 | tf_op jit(solution)/shard_map/all_to_all | solution.py:494
  8.7 0.7 copy-start.2
  8.7 0.7 copy-start.1
  22.1 26.8 %all-to-all-start.1 = ((f32[32,8,128]{2,1,0:T(8,128)}), f32[32,8,128]{2,1,0:T(8,128)S(1)}, u32[]{:S(2)}, u32[]{:S(2)}) async-start(f32[32,8,128]{2,1,0:T(8,128)} %terms_first.1), calls=%async_computation.1 | async-start | bytes 262144 | tf_op jit(solution)/shard_map/all_to_all | solution.py:494
  55.6 25.7 %copy-start = (f32[16,128]{1,0:T(8,128)S(1)}, f32[16,128]{1,0:T(8,128)}, u32[]{:S(2)}) copy-start(f32[16,128]{1,0:T(8,128)} %get-tuple-element.8.rows_ref) | copy-start | bytes 24580
